TPU v7x, 32 devices: a whole 2x2x4 slice. The times are simulated.
32 devices in a mesh: rep: 2 (over y), gx: 16 (over z, x, core).
Axes of the slice: x: 2, y: 2, z: 4, core: 2. Of those that a mesh axis runs over, the one named last changes fastest.
Arguments:
- positions: float32 [3, 49152], P(None, ('rep', 'gx')), parts along dimension 1, may hold values from 0 to 96
- velocities: float32 [3, 49152], P(None, ('rep', 'gx')), parts along dimension 1, may hold values from -9 to 9
- atom_params: float32 [4, 49152], P(None, ('rep', 'gx')), parts along dimension 1, may hold values from -1 to 2, as said below
- pair_list: int32 [3, 540672], P(None, ('rep', 'gx')), parts along dimension 1, may hold values from 0 to 479, as said below
- pair_count: int32 [32], P(('rep', 'gx')), parts along dimension 0, may hold values from 2112 to 16896, as said below
- exclusion: int32 [4, 540672], P(None, ('rep', 'gx')), parts along dimension 1, may hold values from 0 to 65535, as said below
- halo_far: int32 [3072], P(('rep', 'gx')), parts along dimension 0, may hold values from 0 to 191, as said below
- box_lengths: float32 [6], P('rep'), parts along dimension 0, may hold values from 12 to 96
- extended_variables: float32 [8], P('rep'), parts along dimension 0, may hold values from -0.3 to 0.3
Outputs:
- forces: float32 [3, 49152], P(None, ('rep', 'gx')), parts along dimension 1
- new_velocities: float32 [3, 49152], P(None, ('rep', 'gx')), parts along dimension 1
- new_positions: float32 [3, 49152], P(None, ('rep', 'gx')), parts along dimension 1
- new_coupling: float32 [8], P('rep'), parts along dimension 0
There are 2 independent parts, one for each index of `rep`. A program takes and returns all parts, laid end to end along the dimension named above; each array names one. Nothing has to cross between parts.
Inputs may be any that keep to these rules, and one draw needn't show every extreme that they name: `pair_list`: row 0 is a local cluster 0 to 191, row 1 a slot 0 to 479 of the slot table, row 2 an image code 0 to 8. Over each domain's used columns row 0 never falls (the list is grouped by its first cluster). Unused columns hold valid entries too. `pair_count`: at most 16896; some domain uses all 16896 columns in every draw. `exclusion`: each word holds 16 bits; bit 1 means the atom pair interacts. `halo_far`: 96 distinct local clusters of each domain. `atom_params`: rows 1 to 3 are positive.
All inputs are finite; a program needn't handle non-finite values.
Results may differ from a plain program's by a relative error of at most 0.0003.
Values sent between devices are 32-bit elements; how exact they have to be, the bound alone decides.
A program may use at most 64 MiB of HBM per device.

v0:
```python
import functools

import jax
import jax.numpy as jnp
from jax import lax
from jax.experimental import pallas as pl
from jax.experimental.pallas import tpu as pltpu
from jax.sharding import PartitionSpec as P

time_step = 0.25
reaction_term = 1.0 / 1331.0
thermal_scale_unit = 2.0
reservoir_inertia_mass = 4.0
barostat_gain = 0.1
pressure_target = 1.0

LANES = 128


def round_up(value, unit):
    return (value + unit - 1) // unit * unit


def split_three(value):
    high = value.astype(jnp.bfloat16).astype(jnp.float32)
    rest = value - high
    middle = rest.astype(jnp.bfloat16).astype(jnp.float32)
    return jnp.concatenate([high, middle, rest - middle], axis=0).astype(jnp.bfloat16)


def one_hot_rows(index_row, rows, ramp):
    pieces = []
    for base in range(0, rows, 256):
        height = min(256, rows - base)
        moved = (index_row - base).astype(jnp.float32)
        moved = jnp.broadcast_to(moved, (16, LANES)).astype(jnp.bfloat16)
        for first in range(0, height, 16):
            hit = moved == ramp[first : first + 16]
            pieces.append(jnp.where(hit, jnp.bfloat16(1), jnp.bfloat16(0)))
    return jnp.concatenate(pieces, axis=0)


def gathered(table_ref, index_row, tiles):
    index = jnp.broadcast_to(index_row, (8, LANES))
    within = index & (LANES - 1)
    block = index // LANES
    result = []
    for component in range(6):
        value = None
        for tile in range(tiles):
            source = table_ref[component * 8 : component * 8 + 8, tile * LANES : (tile + 1) * LANES]
            picked = jnp.take_along_axis(source, within, axis=1, mode="promise_in_bounds")
            value = picked if value is None else jnp.where(block == tile, picked, value)
        result.append(value)
    return result


def pair_kernel(
    count_ref, box_ref, lift_ref, here_ref, near_ref, beyond_ref, chosen_ref, velocity_ref,
    param_ref, pair_ref, word_ref, own_out, near_out, far_out, sum_ref,
    table_ref, wide_ref, virial_ref, first_got, second_got, bits_got, first_terms, second_terms,
    own_ref, other_ref, *, clusters, slots, block
):
    sublane = lax.broadcasted_iota(jnp.int32, (8, LANES), 0)
    lane = lax.broadcasted_iota(jnp.int32, (8, LANES), 1)
    ramp = lax.broadcasted_iota(jnp.int32, (256, LANES), 0).astype(jnp.float32).astype(jnp.bfloat16)
    count = count_ref[0]
    box_y = box_ref[1]
    box_z = box_ref[2]
    first_tiles = -(-clusters // LANES)
    second_tiles = -(-slots // LANES)
    near_lift = jnp.where(lift_ref[0] >= 1, box_ref[0], 0.0)
    far_lift = jnp.where(lift_ref[0] >= 0, box_ref[0], 0.0)
    upper = lax.broadcasted_iota(jnp.int32, (48, clusters), 0) < 8
    tail = slots - slots % LANES
    if tail < table_ref.shape[1]:
        table_ref[:, tail:] = jnp.zeros((48, table_ref.shape[1] - tail), jnp.float32)
    table_ref[:, 0:clusters] = here_ref[...]
    table_ref[:, clusters : 2 * clusters] = near_ref[...] + jnp.where(upper, near_lift, 0.0)
    wide_ref[...] = jnp.zeros_like(wide_ref)
    wide_ref[:, 0:clusters] = beyond_ref[...]
    far_count = slots - 2 * clusters
    for start in range(0, far_count, LANES):
        width = min(LANES, far_count - start)
        values = gathered(wide_ref, chosen_ref[0:1, start : start + LANES], first_tiles)
        values[0] = values[0] + far_lift
        for component in range(6):
            table_ref[
                component * 8 : component * 8 + 8, 2 * clusters + start : 2 * clusters + start + width
            ] = values[component][:, :width]
    own_ref[...] = jnp.zeros_like(own_ref)
    other_ref[...] = jnp.zeros_like(other_ref)
    virial_ref[...] = jnp.zeros_like(virial_ref)
    first_terms[...] = jnp.zeros_like(first_terms)
    second_terms[...] = jnp.zeros_like(second_terms)

    def fetch(number, part):
        at = pl.multiple_of(number * block + part * LANES, LANES)
        here = pl.ds(at, LANES)
        lanes = slice(part * LANES, (part + 1) * LANES)
        image = jnp.broadcast_to(pair_ref[2:3, here], (8, LANES))
        first = gathered(table_ref, pair_ref[0:1, here], first_tiles)
        second = gathered(table_ref, pair_ref[1:2, here], second_tiles)
        step_y = jnp.where(image >= 6, 1.0, jnp.where(image >= 3, 0.0, -1.0))
        step_z = image.astype(jnp.float32) - 3.0 * step_y - 4.0
        shift = (None, step_y * box_y, step_z * box_z)
        for c in range(3):
            origin = jnp.broadcast_to(first[c][0:1], (8, LANES))
            second[c] = second[c] - origin
            if shift[c] is not None:
                second[c] = second[c] + shift[c]
            first[c] = first[c] - origin
        words = [jnp.broadcast_to(word_ref[w : w + 1, here], (8, LANES)) for w in range(4)]
        low = jnp.where(sublane < 2, words[0], words[1])
        high = jnp.where(sublane < 6, words[2], words[3])
        bits = jnp.where(sublane < 4, low, high) >> (8 * (sublane & 1))
        bits_got[:, lanes] = jnp.where(at + lane < count, bits, 0)
        first[4] = 6.0 * first[4]
        first[5] = 12.0 * first[5]
        for c in range(6):
            first_got[c * 8 : c * 8 + 8, lanes] = first[c]
            second_got[c * 8 : c * 8 + 8, lanes] = second[c]

    def interact(part):
        lanes = slice(part * LANES, (part + 1) * LANES)
        first = [first_got[c * 8 : c * 8 + 8, lanes] for c in range(6)]
        second = [second_got[c * 8 : c * 8 + 8, lanes] for c in range(6)]
        bits = bits_got[:, lanes]
        charge, dispersion, repulsion = first[3], first[4], first[5]
        moving = second
        onto_first = [None] * 3
        onto_second = [None] * 3
        for turn in range(7, -1, -1):
            moving = [pltpu.roll(m, 1, 0) for m in moving] if turn else second
            delta = [moving[c] - first[c] for c in range(3)]
            radius_sq = delta[0] * delta[0] + delta[1] * delta[1] + delta[2] * delta[2]
            inverse = lax.rsqrt(radius_sq)
            inverse_sq = inverse * inverse
            cube = inverse * inverse_sq
            six = cube * cube
            scalar = charge * moving[3] * (cube - reaction_term) + (
                repulsion * moving[5] * six - dispersion * moving[4]
            ) * (six * inverse_sq)
            wanted = (bits & (1 << ((sublane + turn) & 7))) != 0
            scalar = jnp.where(wanted, scalar, 0.0)
            for c in range(3):
                force = scalar * delta[c]
                if onto_first[c] is None:
                    onto_first[c] = -force
                    onto_second[c] = force
                else:
                    onto_first[c] = onto_first[c] - force
                    onto_second[c] = pltpu.roll(onto_second[c], 1, 0) + force
        first_terms[:, lanes] = split_three(jnp.concatenate(onto_first, axis=0))
        second_terms[:, lanes] = split_three(jnp.concatenate(onto_second, axis=0))
        return [onto_second[c] * second[c] + onto_first[c] * first[c] for c in range(3)]

    def spread(number):
        first_hot = []
        second_hot = []
        for part in range(block // LANES):
            here = pl.ds(pl.multiple_of(number * block + part * LANES, LANES), LANES)
            first_hot.append(one_hot_rows(pair_ref[0:1, here], clusters, ramp))
            second_hot.append(one_hot_rows(pair_ref[1:2, here], slots, ramp))
        contract = (((1,), (1,)), ((), ()))
        own_ref[...] += lax.dot_general(
            first_terms[...], jnp.concatenate(first_hot, axis=1), contract,
            preferred_element_type=jnp.float32,
        )
        other_ref[...] += lax.dot_general(
            second_terms[...], jnp.concatenate(second_hot, axis=1), contract,
            preferred_element_type=jnp.float32,
        )

    blocks = jnp.maximum((count + block - 1) // block, 1)
    for part in range(block // LANES):
        fetch(0, part)

    def one_block(number, carry):
        spread(jnp.maximum(number - 1, 0))
        upcoming = jnp.minimum(number + 1, blocks - 1)
        virial = [virial_ref[c * 8 : c * 8 + 8, :] for c in range(3)]
        for part in range(block // LANES):
            added = interact(part)
            virial = [virial[c] + added[c] for c in range(3)]
            fetch(upcoming, part)
        for c in range(3):
            virial_ref[c * 8 : c * 8 + 8, :] = virial[c]
        return carry

    lax.fori_loop(0, blocks, one_block, 0)
    spread(blocks - 1)
    other = other_ref[0:24, :] + other_ref[24:48, :] + other_ref[48:72, :]
    own_out[...] = own_ref[0:24, :] + own_ref[24:48, :] + own_ref[48:72, :] + other[:, 0:clusters]
    near_out[...] = other[:, clusters : 2 * clusters]
    far_sum = jnp.zeros((72, clusters), jnp.float32)
    for start in range(0, far_count, LANES):
        width = min(LANES, far_count - start)
        piece = other[:, 2 * clusters + start : 2 * clusters + start + width]
        if width < LANES:
            piece = jnp.concatenate([piece, jnp.zeros((24, LANES - width), jnp.float32)], axis=1)
        far_sum = far_sum + lax.dot_general(
            split_three(piece),
            one_hot_rows(chosen_ref[0:1, start : start + LANES], clusters, ramp),
            (((1,), (1,)), ((), ())), preferred_element_type=jnp.float32,
        )
    far_out[...] = far_sum[0:24] + far_sum[24:48] + far_sum[48:72]
    energy = velocity_ref[...] * velocity_ref[...] / param_ref[3:4, :]
    energy = 0.5 * jnp.sum(energy, axis=1, keepdims=True)
    rows = [
        jnp.sum(jnp.sum(virial_ref[c * 8 : c * 8 + 8, :], axis=0, keepdims=True), axis=1, keepdims=True) * -0.5
        for c in range(3)
    ]
    rows = rows + [energy, jnp.zeros((2, 1), jnp.float32)]
    sum_ref[...] = jnp.broadcast_to(jnp.concatenate(rows, axis=0), (8, LANES))


def pair_forces(scalars, arrays, pair_list, exclusion, clusters, slots):
    pairs = pair_list.shape[1]
    block = next(b for b in (512, 384, 256, 128) if pairs % b == 0)
    vmem = pl.BlockSpec(memory_space=pltpu.VMEM)
    smem = pl.BlockSpec(memory_space=pltpu.SMEM)
    folded = jax.ShapeDtypeStruct((24, clusters), jnp.float32)
    return pl.pallas_call(
        functools.partial(pair_kernel, clusters=clusters, slots=slots, block=block),
        name="pair_kernel",
        out_shape=(folded, folded, folded, jax.ShapeDtypeStruct((8, LANES), jnp.float32)),
        in_specs=[smem] * 3 + [vmem] * 8,
        out_specs=(vmem,) * 4,
        scratch_shapes=[
            pltpu.VMEM((48, round_up(slots, LANES)), jnp.float32),
            pltpu.VMEM((48, round_up(clusters, LANES)), jnp.float32),
            pltpu.VMEM((24, LANES), jnp.float32),
            pltpu.VMEM((48, block), jnp.float32),
            pltpu.VMEM((48, block), jnp.float32),
            pltpu.VMEM((8, block), jnp.int32),
            pltpu.VMEM((72, block), jnp.bfloat16),
            pltpu.VMEM((72, block), jnp.bfloat16),
            pltpu.VMEM((72, clusters), jnp.float32),
            pltpu.VMEM((72, slots), jnp.float32),
        ],
    )(*scalars, *arrays, pair_list, exclusion)


def final_kernel(
    own_ref, near_ref, far_ref, rate_ref, position_ref, velocity_ref, param_ref,
    force_out, velocity_out, position_out, coupling_out, folded_ref, *, clusters
):
    sublane = lax.broadcasted_iota(jnp.int32, (8, LANES), 0)
    lane = lax.broadcasted_iota(jnp.int32, (8, LANES), 1)
    wanted = sublane == (lane & 7)
    folded_ref[...] = jnp.zeros_like(folded_ref)
    folded_ref[:, 0:clusters] = own_ref[...] + near_ref[...] + far_ref[...]
    for c in range(3):
        for tile in range(clusters * 8 // LANES):
            at = tile * 16
            source = folded_ref[c * 8 : c * 8 + 8, at // LANES * LANES : at // LANES * LANES + LANES]
            picked = jnp.take_along_axis(
                source, at % LANES + lane // 8, axis=1, mode="promise_in_bounds"
            )
            force_out[c : c + 1, tile * LANES : (tile + 1) * LANES] = jnp.sum(
                jnp.where(wanted, picked, 0.0), axis=0, keepdims=True
            )
    row = jnp.broadcast_to(rate_ref[3:4, :], (1, LANES))
    for c in range(3):
        row = jnp.where(lane[0:1] == c + 1, rate_ref[c : c + 1, :], row)
    coupling_out[...] = row[:, 0:4]
    rates = rate_ref[0:3, 0:1]
    damping = rate_ref[3:4, 0:1]
    velocity = velocity_ref[...]
    moved = velocity + time_step * (
        force_out[...] * param_ref[3:4, :] - (damping + rates) * velocity
    )
    velocity_out[...] = moved
    position_out[...] = position_ref[...] * (1.0 + time_step * rates) + time_step * moved


def finished(own, near_back, far_back, rates, positions, velocities, atom_params):
    vmem = pl.BlockSpec(memory_space=pltpu.VMEM)
    clusters = own.shape[1]
    shape = jax.ShapeDtypeStruct(positions.shape, jnp.float32)
    return pl.pallas_call(
        functools.partial(final_kernel, clusters=clusters),
        name="final_kernel",
        out_shape=(shape,) * 3 + (jax.ShapeDtypeStruct((1, 4), jnp.float32),),
        in_specs=[vmem] * 7,
        out_specs=(vmem,) * 4,
        scratch_shapes=[pltpu.VMEM((24, round_up(clusters, LANES)), jnp.float32)],
    )(own, near_back, far_back, rates, positions, velocities, atom_params)


def pack_kernel(position_ref, param_ref, halo_ref, packed_out, chosen_out, *, clusters, far):
    sublane = lax.broadcasted_iota(jnp.int32, (8, LANES), 0)
    lane = lax.broadcasted_iota(jnp.int32, (8, LANES), 1)
    place = (lane & 15) * 8 + sublane
    for component in range(6):
        source = position_ref if component < 3 else param_ref
        row = component % 3
        for start in range(0, clusters, LANES):
            width = min(LANES, clusters - start)
            value = jnp.zeros((8, LANES), jnp.float32)
            for piece in range(width // 16):
                at = start * 8 + piece * LANES
                spread = jnp.broadcast_to(source[row : row + 1, at : at + LANES], (8, LANES))
                picked = jnp.take_along_axis(spread, place, axis=1, mode="promise_in_bounds")
                value = jnp.where(lane // 16 == piece, picked, value)
            packed_out[component * 8 : component * 8 + 8, start : start + width] = value[:, :width]
    chosen_out[...] = jnp.zeros_like(chosen_out)
    chosen_out[:, 0:far] = halo_ref[...]


def pack(positions, atom_params, halo_far):
    vmem = pl.BlockSpec(memory_space=pltpu.VMEM)
    clusters = positions.shape[1] // 8
    far = halo_far.shape[0]
    return pl.pallas_call(
        functools.partial(pack_kernel, clusters=clusters, far=far),
        name="pack_kernel",
        out_shape=(
            jax.ShapeDtypeStruct((48, clusters), jnp.float32),
            jax.ShapeDtypeStruct((1, round_up(far, LANES)), jnp.int32),
        ),
        in_specs=[vmem] * 3,
        out_specs=(vmem,) * 2,
    )(positions, atom_params, halo_far[None, :])


def send(source, target, sems, place, device):
    return pltpu.make_async_remote_copy(
        src_ref=source,
        dst_ref=target,
        send_sem=sems[0].at[place],
        recv_sem=sems[1].at[place],
        device_id={"gx": device},
        device_id_type=pl.DeviceIdType.MESH,
    )


def forward_kernel(packed_ref, chosen_ref, near_ref, beyond_ref, picked_ref, send_sems, recv_sems, *, count):
    me = lax.axis_index("gx")
    barrier = pltpu.get_barrier_semaphore()
    for step in (1, 2, count - 1, count - 2):
        pl.semaphore_signal(
            barrier, inc=1, device_id={"gx": lax.rem(me + step, count)},
            device_id_type=pl.DeviceIdType.MESH,
        )
    pl.semaphore_wait(barrier, 4)
    below = lax.rem(me + count - 1, count)
    far_below = lax.rem(me + count - 2, count)
    sems = (send_sems, recv_sems)
    copies = [
        send(packed_ref, beyond_ref, sems, 1, far_below),
        send(chosen_ref, picked_ref, sems, 2, far_below),
        send(packed_ref, near_ref, sems, 0, below),
    ]
    for copy in copies:
        copy.start()
    for copy in copies:
        copy.wait()


def forward(packed, chosen, count):
    vmem = pl.BlockSpec(memory_space=pltpu.VMEM)
    return pl.pallas_call(
        functools.partial(forward_kernel, count=count),
        name="forward_kernel",
        out_shape=(
            jax.ShapeDtypeStruct(packed.shape, packed.dtype),
            jax.ShapeDtypeStruct(packed.shape, packed.dtype),
            jax.ShapeDtypeStruct(chosen.shape, chosen.dtype),
        ),
        in_specs=[vmem] * 2,
        out_specs=(vmem,) * 3,
        scratch_shapes=[pltpu.SemaphoreType.DMA((3,)), pltpu.SemaphoreType.DMA((3,))],
        compiler_params=pltpu.CompilerParams(collective_id=0, has_side_effects=True),
    )(packed, chosen)


def return_kernel(
    box_ref, extended_ref, near_ref, far_ref, sum_ref, near_back, far_back, rate_ref,
    all_sums, send_sems, recv_sems, give_sems, take_sems, *, count, particles
):
    me = lax.axis_index("gx")
    barrier = pltpu.get_barrier_semaphore()

    def greet(step, carry):
        pl.semaphore_signal(
            barrier, inc=1, device_id={"gx": lax.rem(me + step, count)},
            device_id_type=pl.DeviceIdType.MESH,
        )
        return carry

    lax.fori_loop(1, count, greet, 0)
    pl.semaphore_wait(barrier, count - 1)
    sems = (send_sems, recv_sems)
    copies = [
        send(far_ref, far_back, sems, 1, lax.rem(me + 2, count)),
        send(near_ref, near_back, sems, 0, lax.rem(me + 1, count)),
    ]

    def sum_copy(step, source):
        return pltpu.make_async_remote_copy(
            src_ref=sum_ref,
            dst_ref=all_sums.at[source],
            send_sem=give_sems.at[step],
            recv_sem=take_sems.at[source],
            device_id={"gx": lax.rem(me + step, count)},
            device_id_type=pl.DeviceIdType.MESH,
        )

    def give(step, carry):
        sum_copy(step, me).start()
        return carry

    def take(step, carry):
        sum_copy(step, lax.rem(me + count - step, count)).wait()
        return carry

    lax.fori_loop(1, count, give, 0)
    for copy in copies:
        copy.start()
    all_sums[me] = sum_ref[...]
    lax.fori_loop(1, count, take, 0)
    total = lax.fori_loop(
        0, count, lambda source, held: held + all_sums[source], jnp.zeros((8, LANES), jnp.float32)
    )
    virial = total[0:3]
    kinetic = total[3:6]
    energy = total[3:4] + total[4:5] + total[5:6]
    volume = box_ref[0] * box_ref[1] * box_ref[2]
    ratio = 2.0 * energy / (3.0 * particles * thermal_scale_unit)
    rate_ref[3:4] = extended_ref[0] + reservoir_inertia_mass * (ratio - 1.0)
    change = barostat_gain * (kinetic - virial - pressure_target * volume / 2.0) / (energy / 3.0)
    for c in range(3):
        rate_ref[c : c + 1] = extended_ref[1 + c] + change[c : c + 1]
    for copy in copies:
        copy.wait()


def returned(box_lengths, extended_variables, near, far, sums, count, particles):
    vmem = pl.BlockSpec(memory_space=pltpu.VMEM)
    smem = pl.BlockSpec(memory_space=pltpu.SMEM)
    return pl.pallas_call(
        functools.partial(return_kernel, count=count, particles=particles),
        name="return_kernel",
        out_shape=(
            jax.ShapeDtypeStruct(near.shape, near.dtype),
            jax.ShapeDtypeStruct(far.shape, far.dtype),
            jax.ShapeDtypeStruct((4, LANES), jnp.float32),
        ),
        in_specs=[smem] * 2 + [vmem] * 3,
        out_specs=(vmem,) * 3,
        scratch_shapes=[
            pltpu.VMEM((count, 8, LANES), jnp.float32),
            pltpu.SemaphoreType.DMA((2,)),
            pltpu.SemaphoreType.DMA((2,)),
            pltpu.SemaphoreType.DMA((count,)),
            pltpu.SemaphoreType.DMA((count,)),
        ],
        compiler_params=pltpu.CompilerParams(collective_id=1, has_side_effects=True),
    )(box_lengths, extended_variables, near, far, sums)


def on_device(
    positions,
    velocities,
    atom_params,
    pair_list,
    pair_count,
    exclusion,
    halo_far,
    box_lengths,
    extended_variables,
):
    atoms_here = positions.shape[1]
    clusters = atoms_here // 8
    far_clusters = halo_far.shape[0]
    slots = 2 * clusters + far_clusters
    axis_count = lax.axis_size("gx")
    packed, chosen = pack(positions, atom_params, halo_far)
    near_rows, beyond, picked = forward(packed, chosen, axis_count)
    lift = (lax.axis_index("gx") - (axis_count - 2)).astype(jnp.int32)[None]
    own, near, far, sums = pair_forces(
        (pair_count, box_lengths, lift),
        (packed, near_rows, beyond, picked, velocities, atom_params),
        pair_list, exclusion, clusters, slots,
    )
    near_back, far_back, rates = returned(
        box_lengths, extended_variables, near, far, sums, axis_count, atoms_here * axis_count
    )
    forces, new_velocities, new_positions, new_coupling = finished(
        own, near_back, far_back, rates, positions, velocities, atom_params
    )
    return (forces, new_velocities, new_positions, new_coupling.reshape(4))


def solution(mesh):
    return jax.shard_map(
        on_device,
        mesh=mesh,
        in_specs=(
            P(None, ("rep", "gx")),
            P(None, ("rep", "gx")),
            P(None, ("rep", "gx")),
            P(None, ("rep", "gx")),
            P(("rep", "gx")),
            P(None, ("rep", "gx")),
            P(("rep", "gx")),
            P("rep"),
            P("rep"),
        ),
        out_specs=(
            P(None, ("rep", "gx")),
            P(None, ("rep", "gx")),
            P(None, ("rep", "gx")),
            P("rep"),
        ),
        check_vma=False,
    )
```

profile of v0, /device:TPU:0, one launch (start us, length us, event | category | flops | bytes accessed | tf_op | source)
XLA Modules:
  0.0 38.1 jit_solution(9343904956236222319)
XLA Ops:
  1.3 1.5 %pack_kernel.1 = (f32[48,192]{1,0:T(8,128)}, s32[1,128]{1,0:T(1,128)}) custom-call(f32[3,1536]{1,0:T(4,128)} %position_ref.3, f32[4,1536]{1,0:T(4,128)} %param_ref.5, s32[1,96]{1,0:T(1,128)} %bitcast.3), custom_call_target="tpu_custom_call" | custom-call | tf_op jit(solution)/shard_map/pack_kernel/pallas_call | solution.py:316
  2.8 9.7 %forward_kernel.1 = (f32[48,192]{1,0:T(8,128)}, f32[48,192]{1,0:T(8,128)}, s32[1,128]{1,0:T(1,128)}) custom-call(f32[48,192]{1,0:T(8,128)} %get-tuple-element.20.packed_ref.here_ref, s32[1,128]{1,0:T(1,128)} %get-tuple-element.21.chosen_ref), custom_call_target="tpu_custom_call" | custom-call | tf_op jit(solution)/shard_map/forward_kernel/pallas_call | solution.py:364
  12.5 5.0 %pair_kernel.1 = (f32[24,192]{1,0:T(8,128)}, f32[24,192]{1,0:T(8,128)}, f32[24,192]{1,0:T(8,128)}, f32[8,128]{1,0:T(8,128)}) custom-call(s32[1]{0:T(128)S(6)} %copy.13.count_ref, f32[3]{0:T(128)} %box_ref.3, s32[1]{0:T(128)} %bitcast.lift_ref, f32[48,192]{1,0:T(8,128)} %get-tuple-element.20.packed_ref.here_ref, f32[48,192]{1,0:T(8,128)} %get-tuple-element.22.near_ref, ...), custom_call_target="tpu_custom_call" | custom-call | tf_op jit(solution)/shard_map/pair_kernel/pallas_call | solution.py:224
  17.5 18.9 %return_kernel.1 = (f32[24,192]{1,0:T(8,128)}, f32[24,192]{1,0:T(8,128)}, f32[4,128]{1,0:T(4,128)}) custom-call(f32[3]{0:T(128)} %box_ref.3, f32[4]{0:T(128)} %extended_ref.1, f32[24,192]{1,0:T(8,128)} %get-tuple-element.26.near_ref, f32[24,192]{1,0:T(8,128)} %get-tuple-element.27.far_ref, f32[8,128]{1,0:T(8,128)} %get-tuple-element.28.sum_ref), custom_call_target="tpu_custom_call" | custom-call | tf_op jit(solution)/shard_map/return_kernel/pallas_call | solution.py:443
  36.5 1.6 %final_kernel.1 = (f32[3,1536]{1,0:T(4,128)}, f32[3,1536]{1,0:T(4,128)}, f32[3,1536]{1,0:T(4,128)}, f32[1,4]{1,0:T(1,128)}) custom-call(f32[24,192]{1,0:T(8,128)} %get-tuple-element.25.own_ref, f32[24,192]{1,0:T(8,128)} %get-tuple-element.29.near_ref, f32[24,192]{1,0:T(8,128)} %get-tuple-element.30.far_ref, f32[4,128]{1,0:T(4,128)} %get-tuple-element.31.rate_ref, ...), custom_call_target="tpu_custom_call" | custom-call | tf_op jit(solution)/shard_map/final_kernel/pallas_call | solution.py:282
where the time goes:
time: 38.4 us; the launch traced here: 38.1 us
  Pallas kernels  36.8 us (96%)
  between operations  1.3 us (3%)
    pallas_call x1, Pallas kernels, returned(): pl.pallas_call(functools.partial(return_kernel, count=count, particles=pa...  18.9 us
    pallas_call x1, Pallas kernels, forward(): pl.pallas_call(functools.partial(forward_kernel, count=count), name='forw...  9.71 us
    pallas_call x1, Pallas kernels, pair_forces(): pl.pallas_call(functools.partial(pair_kernel, clusters=clusters, slots=sl...  5.01 us
    pallas_call x1, Pallas kernels, finished(): pl.pallas_call(functools.partial(final_kernel, clusters=clusters), name='...  1.65 us
    pallas_call x1, Pallas kernels, pack(): pl.pallas_call(functools.partial(pack_kernel, clusters=clusters, far=far)...  1.52 us

commit v1 on v0

v1 whole, which is shorter than its diff:
```python
import functools

import jax
import jax.numpy as jnp
from jax import lax
from jax.experimental import pallas as pl
from jax.experimental.pallas import tpu as pltpu
from jax.sharding import PartitionSpec as P

time_step = 0.25
reaction_term = 1.0 / 1331.0
thermal_scale_unit = 2.0
reservoir_inertia_mass = 4.0
barostat_gain = 0.1
pressure_target = 1.0

LANES = 128
FAR_AWAY = 1e36


def round_up(value, unit):
    return (value + unit - 1) // unit * unit


def split_two(parts):
    value = jnp.concatenate(parts, axis=0)
    high = value.astype(jnp.bfloat16)
    low = (value - high.astype(jnp.float32)).astype(jnp.bfloat16)
    return jnp.concatenate([high, low], axis=0)


def picked_rows(table_ref, index, first_tile, last_tile, held=None):
    within = index & (LANES - 1)
    block = index // LANES
    result = []
    for component in range(6):
        value = None if held is None else held[component]
        for tile in range(first_tile, last_tile):
            source = table_ref[component * 8 : component * 8 + 8, tile * LANES : (tile + 1) * LANES]
            picked = jnp.take_along_axis(source, within, axis=1, mode="promise_in_bounds")
            value = picked if value is None else jnp.where(block == tile, picked, value)
        result.append(value)
    return result


def step_kernel(
    box_ref, extended_ref, count_ref, position_in, velocity_in, param_in, pair_in, word_in, halo_in,
    force_out, velocity_out, position_out, coupling_out,
    position_ref, velocity_ref, param_ref, pair_ref, word_ref, halo_ref,
    table_ref, packed_ref, near_got, far_send, far_got, near_push, far_push, near_back, far_back,
    sum_ref, all_sums, place_ref, folded_ref,
    first_kept, far_kept, term_kept, first_hot, second_hot,
    second_got, first_terms, second_terms, own_ref, other_ref, virial_ref,
    local_sems, send_sems, recv_sems, give_sems, take_sems,
    *, count, clusters, slots, block
):
    me = lax.axis_index("gx")
    parts = block // LANES
    pairs = pair_ref.shape[1]
    blocks = pairs // block
    far_count = slots - 2 * clusters
    first_tiles = -(-clusters // LANES)
    second_tiles = -(-slots // LANES)
    barrier = pltpu.get_barrier_semaphore()

    def greet(step, carry):
        pl.semaphore_signal(
            barrier, inc=1, device_id={"gx": lax.rem(me + step, count)},
            device_id_type=pl.DeviceIdType.MESH,
        )
        return carry

    lax.fori_loop(1, count, greet, 0)
    inward = [
        pltpu.make_async_copy(source, target, local_sems.at[number])
        for number, (source, target) in enumerate((
            (position_in, position_ref), (param_in, param_ref), (halo_in, halo_ref),
            (pair_in, pair_ref), (word_in, word_ref), (velocity_in, velocity_ref),
        ))
    ]
    for copy in inward:
        copy.start()

    sublane = lax.broadcasted_iota(jnp.int32, (8, LANES), 0)
    lane = lax.broadcasted_iota(jnp.int32, (8, LANES), 1)
    own_ref[...] = jnp.zeros_like(own_ref)
    other_ref[...] = jnp.zeros_like(other_ref)
    virial_ref[...] = jnp.zeros_like(virial_ref)
    first_terms[...] = jnp.zeros_like(first_terms)
    second_terms[...] = jnp.zeros_like(second_terms)
    packed_ref[...] = jnp.zeros_like(packed_ref)
    table_ref[...] = jnp.zeros_like(table_ref)

    for copy in inward[:3]:
        copy.wait()
    place = (lane & 15) * 8 + sublane
    for component in range(6):
        source = position_ref if component < 3 else param_ref
        row = component % 3
        for start in range(0, clusters, LANES):
            width = min(LANES, clusters - start)
            value = jnp.zeros((8, LANES), jnp.float32)
            for piece in range(width // 16):
                at = start * 8 + piece * LANES
                spread = jnp.broadcast_to(source[row : row + 1, at : at + LANES], (8, LANES))
                picked = jnp.take_along_axis(spread, place, axis=1, mode="promise_in_bounds")
                value = jnp.where(lane // 16 == piece, picked, value)
            packed_ref[component * 8 : component * 8 + 8, start : start + LANES] = value
    for start in range(0, far_count, LANES):
        width = min(LANES, far_count - start)
        chosen = halo_ref[0:1, start : start + width]
        if width < LANES:
            chosen = jnp.concatenate([chosen, jnp.zeros((1, LANES - width), jnp.int32)], axis=1)
        values = picked_rows(packed_ref, jnp.broadcast_to(chosen, (8, LANES)), 0, first_tiles)
        for component in range(6):
            far_send[component * 8 : component * 8 + 8, start : start + LANES] = values[component]
    table_ref[:, 0:clusters] = packed_ref[:, 0:clusters]

    def remote(source, target, number, hops):
        return pltpu.make_async_remote_copy(
            src_ref=source, dst_ref=target,
            send_sem=send_sems.at[number], recv_sem=recv_sems.at[number],
            device_id={"gx": lax.rem(me + hops, count)}, device_id_type=pl.DeviceIdType.MESH,
        )

    pl.semaphore_wait(barrier, count - 1)
    outward = [remote(far_send, far_got, 1, count - 2), remote(packed_ref, near_got, 0, count - 1)]
    for copy in outward:
        copy.start()
    for copy in inward[3:]:
        copy.wait()

    total = count_ref[0]
    pair_lane = lax.broadcasted_iota(jnp.int32, (16, LANES), 1)

    def hot(column, width, target, at):
        index = jnp.broadcast_to(column, (LANES, LANES)).astype(jnp.int16)
        for start in range(0, width, LANES):
            wanted = (lax.broadcasted_iota(jnp.int32, (LANES, LANES), 1) + start).astype(jnp.int16)
            target[pl.ds(at, LANES), start : start + LANES] = jnp.where(
                index == wanted, jnp.bfloat16(1), jnp.bfloat16(0)
            )

    def prepare(number, carry):
        rows = []
        for row in range(2):
            for part in range(parts):
                at = pl.multiple_of(number * block + part * LANES, LANES)
                rows.append(pair_ref[row : row + 1, pl.ds(at, LANES)])
        if len(rows) % 8:
            rows.append(jnp.zeros((8 - len(rows) % 8, LANES), jnp.int32))
        columns = jnp.concatenate(rows, axis=0).T
        for part in range(parts):
            at = pl.multiple_of(number * block + part * LANES, LANES)
            here = pl.ds(at, LANES)
            hot(columns[:, part : part + 1], first_hot.shape[1], first_hot, at)
            hot(columns[:, parts + part : parts + part + 1], second_hot.shape[1], second_hot, at)
            first = picked_rows(
                packed_ref, jnp.broadcast_to(pair_ref[0:1, here], (8, LANES)), 0, first_tiles
            )
            for c in range(3):
                origin = first[c][0:1]
                first_kept[48 + c : 49 + c, here] = origin
                first[c] = first[c] - jnp.broadcast_to(origin, (8, LANES))
            first[4] = 6.0 * first[4]
            first[5] = 12.0 * first[5]
            for c in range(6):
                first_kept[c * 8 : c * 8 + 8, here] = first[c]
            words = [jnp.broadcast_to(word_ref[w : w + 1, here], (8, LANES)) for w in range(4)]
            low = jnp.where(sublane < 2, words[0], words[1])
            high = jnp.where(sublane < 6, words[2], words[3])
            bits = jnp.where(sublane < 4, low, high) >> (8 * (sublane & 1))
            bits = jnp.where(at + lane < total, bits, 0)
            for turn in range(8):
                wanted = (bits & (1 << ((sublane + turn) & 7))) != 0
                rows8 = slice(turn * 8, turn * 8 + 8)
                far_kept[rows8, here] = jnp.where(wanted, 0.0, FAR_AWAY)
                term_kept[rows8, here] = jnp.where(wanted, reaction_term, 0.0)
        return carry

    lax.fori_loop(0, blocks, prepare, 0)
    energy = velocity_ref[...] * velocity_ref[...] / param_ref[3:4, :]
    energy = 0.5 * jnp.sum(energy, axis=1, keepdims=True)
    place_ref[...] = jnp.full_like(place_ref, -1)
    for start in range(0, far_count, LANES):
        width = min(LANES, far_count - start)
        chosen = halo_ref[0:1, start : start + width].astype(jnp.float32)
        for base in range(0, clusters, LANES):
            height = min(LANES, clusters - base)
            wanted = lax.broadcasted_iota(jnp.int32, (LANES, width), 0).astype(jnp.float32) + base
            hit = jnp.where(jnp.broadcast_to(chosen, (LANES, width)) == wanted, 1.0, 0.0)
            column = lax.broadcasted_iota(jnp.int32, (8, width), 1).astype(jnp.float32)
            found = lax.dot_general(
                jnp.concatenate([column + 1.0, jnp.zeros((8, width), jnp.float32)], axis=0).astype(jnp.bfloat16),
                hit.astype(jnp.bfloat16), (((1,), (1,)), ((), ())), preferred_element_type=jnp.float32,
            )[0:8].astype(jnp.int32)
            held = place_ref[:, base : base + LANES]
            place_ref[:, base : base + LANES] = jnp.where(found > 0, found - 1 + start, held)

    for copy in outward:
        copy.wait()
    near_lift = jnp.where(me >= count - 1, box_ref[0], 0.0)
    far_lift = jnp.where(me >= count - 2, box_ref[0], 0.0)
    upper = lax.broadcasted_iota(jnp.int32, (48, clusters), 0) < 8
    table_ref[:, clusters : 2 * clusters] = near_got[:, 0:clusters] + jnp.where(upper, near_lift, 0.0)
    upper = lax.broadcasted_iota(jnp.int32, (48, far_count), 0) < 8
    table_ref[:, 2 * clusters : slots] = far_got[:, 0:far_count] + jnp.where(upper, far_lift, 0.0)
    box_y = box_ref[1]
    box_z = box_ref[2]

    def fetch(number, part):
        at = pl.multiple_of(number * block + part * LANES, LANES)
        here = pl.ds(at, LANES)
        lanes = slice(part * LANES, (part + 1) * LANES)
        image = jnp.broadcast_to(pair_ref[2:3, here], (8, LANES))
        second = picked_rows(
            table_ref, jnp.broadcast_to(pair_ref[1:2, here], (8, LANES)), 0, second_tiles
        )
        step_y = jnp.where(image >= 6, 1.0, jnp.where(image >= 3, 0.0, -1.0))
        step_z = image.astype(jnp.float32) - 3.0 * step_y - 4.0
        shift = (None, step_y * box_y, step_z * box_z)
        for c in range(3):
            second[c] = second[c] - jnp.broadcast_to(first_kept[48 + c : 49 + c, here], (8, LANES))
            if shift[c] is not None:
                second[c] = second[c] + shift[c]
        for c in range(6):
            second_got[c * 8 : c * 8 + 8, lanes] = second[c]

    def interact(number, part):
        here = pl.ds(pl.multiple_of(number * block + part * LANES, LANES), LANES)
        lanes = slice(part * LANES, (part + 1) * LANES)
        first = [first_kept[c * 8 : c * 8 + 8, here] for c in range(6)]
        second = [second_got[c * 8 : c * 8 + 8, lanes] for c in range(6)]
        charge, dispersion, repulsion = first[3], first[4], first[5]
        moving = second
        from_first = [None] * 3
        onto_second = [None] * 3
        for turn in range(7, -1, -1):
            moving = [pltpu.roll(m, 1, 0) for m in moving] if turn else second
            delta = [moving[c] - first[c] for c in range(3)]
            rows8 = slice(turn * 8, turn * 8 + 8)
            radius_sq = delta[0] * delta[0] + delta[1] * delta[1] + delta[2] * delta[2]
            inverse = lax.rsqrt(radius_sq + far_kept[rows8, here])
            inverse_sq = inverse * inverse
            cube = inverse * inverse_sq
            six = cube * cube
            scalar = charge * moving[3] * (cube - term_kept[rows8, here]) + (
                repulsion * moving[5] * six - dispersion * moving[4]
            ) * (six * inverse_sq)
            for c in range(3):
                force = scalar * delta[c]
                if from_first[c] is None:
                    from_first[c] = force
                    onto_second[c] = force
                else:
                    from_first[c] = from_first[c] + force
                    onto_second[c] = pltpu.roll(onto_second[c], 1, 0) + force
        first_terms[:, lanes] = split_two(from_first)
        second_terms[:, lanes] = split_two(onto_second)
        return [onto_second[c] * second[c] - from_first[c] * first[c] for c in range(3)]

    def spread(number):
        here = pl.ds(pl.multiple_of(number * block, LANES), block)
        contract = (((1,), (0,)), ((), ()))
        own_ref[...] += lax.dot_general(
            first_terms[...], first_hot[here, :], contract, preferred_element_type=jnp.float32
        )
        other_ref[...] += lax.dot_general(
            second_terms[...], second_hot[here, :], contract, preferred_element_type=jnp.float32
        )

    for part in range(parts):
        fetch(0, part)

    def one_block(number, carry):
        spread(jnp.maximum(number - 1, 0))
        upcoming = jnp.minimum(number + 1, blocks - 1)
        virial = [virial_ref[c * 8 : c * 8 + 8, :] for c in range(3)]
        for part in range(parts):
            added = interact(number, part)
            virial = [virial[c] + added[c] for c in range(3)]
            fetch(upcoming, part)
        for c in range(3):
            virial_ref[c * 8 : c * 8 + 8, :] = virial[c]
        return carry

    lax.fori_loop(0, blocks, one_block, 0)
    spread(blocks - 1)
    rows = [
        jnp.sum(jnp.sum(virial_ref[c * 8 : c * 8 + 8, :], axis=0, keepdims=True), axis=1, keepdims=True) * -0.5
        for c in range(3)
    ]
    rows = rows + [energy, jnp.zeros((2, 1), jnp.float32)]
    sum_ref[...] = jnp.broadcast_to(jnp.concatenate(rows, axis=0), (8, LANES))

    def sum_copy(step, source):
        return pltpu.make_async_remote_copy(
            src_ref=sum_ref, dst_ref=all_sums.at[source],
            send_sem=give_sems.at[step], recv_sem=take_sems.at[source],
            device_id={"gx": lax.rem(me + step, count)}, device_id_type=pl.DeviceIdType.MESH,
        )

    def give(step, carry):
        sum_copy(step, me).start()
        return carry

    def take(step, carry):
        sum_copy(step, lax.rem(me + count - step, count)).wait()
        return carry

    other = other_ref[0:24, :] + other_ref[24:48, :]
    near_push[:, 0:clusters] = other[:, clusters : 2 * clusters]
    far_push[:, 0:far_count] = other[:, 2 * clusters : slots]
    homeward = [remote(far_push, far_back, 3, 2), remote(near_push, near_back, 2, 1)]
    for copy in homeward:
        copy.start()
    lax.fori_loop(1, count, give, 0)
    all_sums[me] = sum_ref[...]
    folded_ref[:, 0:clusters] = (
        other[:, 0:clusters] - own_ref[0:24, 0:clusters] - own_ref[24:48, 0:clusters]
    )
    for copy in homeward:
        copy.wait()
    place = place_ref[...]
    for base in range(0, clusters, LANES):
        lanes = slice(base, base + LANES)
        index = place[:, lanes]
        within = jnp.maximum(index, 0) & (LANES - 1)
        for c in range(3):
            rows8 = slice(c * 8, c * 8 + 8)
            value = folded_ref[rows8, lanes] + near_back[rows8, lanes]
            for tile in range(-(-far_count // LANES)):
                source = far_back[rows8, tile * LANES : (tile + 1) * LANES]
                picked = jnp.take_along_axis(source, within, axis=1, mode="promise_in_bounds")
                mine = (index >= tile * LANES) & (index < (tile + 1) * LANES)
                value = value + jnp.where(mine, picked, 0.0)
            folded_ref[rows8, lanes] = value
    wanted = sublane == (lane & 7)
    for c in range(3):
        for tile in range(clusters * 8 // LANES):
            at = tile * 16
            source = folded_ref[c * 8 : c * 8 + 8, at // LANES * LANES : at // LANES * LANES + LANES]
            picked = jnp.take_along_axis(
                source, at % LANES + lane // 8, axis=1, mode="promise_in_bounds"
            )
            force_out[c : c + 1, tile * LANES : (tile + 1) * LANES] = jnp.sum(
                jnp.where(wanted, picked, 0.0), axis=0, keepdims=True
            )
    lax.fori_loop(1, count, take, 0)
    totals = lax.fori_loop(
        0, count, lambda source, held: held + all_sums[source], jnp.zeros((8, LANES), jnp.float32)
    )
    virial = totals[0:3]
    kinetic = totals[3:6]
    energy = totals[3:4] + totals[4:5] + totals[5:6]
    volume = box_ref[0] * box_ref[1] * box_ref[2]
    ratio = 2.0 * energy / (3.0 * count * clusters * 8 * thermal_scale_unit)
    damping = extended_ref[0] + reservoir_inertia_mass * (ratio - 1.0)
    change = barostat_gain * (kinetic - virial - pressure_target * volume / 2.0) / (energy / 3.0)
    row = damping
    rates = []
    for c in range(3):
        rates.append(extended_ref[1 + c] + change[c : c + 1])
        row = jnp.where(lane[0:1] == c + 1, rates[c], row)
    coupling_out[...] = row[:, 0:4]
    rates = jnp.concatenate(rates, axis=0)[:, 0:1]
    velocity = velocity_ref[...]
    moved = velocity + time_step * (
        force_out[...] * param_ref[3:4, :] - (damping[:, 0:1] + rates) * velocity
    )
    velocity_out[...] = moved
    position_out[...] = position_ref[...] * (1.0 + time_step * rates) + time_step * moved


def on_device(
    positions,
    velocities,
    atom_params,
    pair_list,
    pair_count,
    exclusion,
    halo_far,
    box_lengths,
    extended_variables,
):
    clusters = positions.shape[1] // 8
    far_clusters = halo_far.shape[0]
    slots = 2 * clusters + far_clusters
    pairs = pair_list.shape[1]
    count = lax.axis_size("gx")
    block = next(b for b in (512, 384, 256, 128) if pairs % b == 0)
    wide = round_up(clusters, LANES)
    wide_far = round_up(far_clusters, LANES)
    wide_slots = round_up(slots, LANES)
    vmem = pl.BlockSpec(memory_space=pltpu.VMEM)
    smem = pl.BlockSpec(memory_space=pltpu.SMEM)
    anywhere = pl.BlockSpec(memory_space=pl.ANY)
    shape = jax.ShapeDtypeStruct(positions.shape, jnp.float32)
    f32 = lambda *dims: pltpu.VMEM(dims, jnp.float32)
    halo = halo_far[None, :]
    forces, new_velocities, new_positions, new_coupling = pl.pallas_call(
        functools.partial(step_kernel, count=count, clusters=clusters, slots=slots, block=block),
        name="step_kernel",
        out_shape=(shape,) * 3 + (jax.ShapeDtypeStruct((1, 4), jnp.float32),),
        in_specs=[smem] * 3 + [anywhere] * 6,
        out_specs=(vmem,) * 4,
        scratch_shapes=[
            f32(*positions.shape), f32(*velocities.shape), f32(*atom_params.shape),
            pltpu.VMEM(pair_list.shape, jnp.int32), pltpu.VMEM(exclusion.shape, jnp.int32),
            pltpu.VMEM(halo.shape, jnp.int32),
            f32(48, wide_slots), f32(48, wide), f32(48, wide), f32(48, wide_far), f32(48, wide_far),
            f32(24, wide), f32(24, wide_far), f32(24, wide), f32(24, wide_far),
            f32(8, LANES), f32(count, 8, LANES),
            pltpu.VMEM((8, wide), jnp.int32), f32(24, wide),
            f32(56, pairs), f32(64, pairs), f32(64, pairs),
            pltpu.VMEM((pairs, wide), jnp.bfloat16), pltpu.VMEM((pairs, wide_slots), jnp.bfloat16),
            f32(48, block), pltpu.VMEM((48, block), jnp.bfloat16), pltpu.VMEM((48, block), jnp.bfloat16),
            f32(48, wide), f32(48, wide_slots), f32(24, LANES),
            pltpu.SemaphoreType.DMA((6,)), pltpu.SemaphoreType.DMA((4,)), pltpu.SemaphoreType.DMA((4,)),
            pltpu.SemaphoreType.DMA((count,)), pltpu.SemaphoreType.DMA((count,)),
        ],
        compiler_params=pltpu.CompilerParams(
            collective_id=0, has_side_effects=True, vmem_limit_bytes=60 * 1024 * 1024
        ),
    )(box_lengths, extended_variables, pair_count, positions, velocities, atom_params, pair_list, exclusion, halo)
    return (forces, new_velocities, new_positions, new_coupling.reshape(4))


def solution(mesh):
    spread = P(None, ("rep", "gx"))
    return jax.shard_map(
        on_device,
        mesh=mesh,
        in_specs=(spread,) * 4 + (P(("rep", "gx")), spread, P(("rep", "gx")), P("rep"), P("rep")),
        out_specs=(spread,) * 3 + (P("rep"),),
        check_vma=False,
    )
```

time: 38.4 us -> 41.2 us (1.073)
  local copies, waits for them, and re-layouts: 0 us -> 3.27 us
    unnamed x0 -> x10, local copies, waits for them, and re-layouts: none -> 3.27 us
    pallas_call x5 -> x1, Pallas kernels: 36.8 us -> 36.4 us  [on_device(): pl.pallas_call(functools.partial(step_kernel, count=count, clusters=clust...]
where the time goes in v1:
time: 41.2 us; the launch traced here: 40.9 us
  Pallas kernels  36.4 us (88%)
  local copies, waits for them, and re-layouts  3.27 us (8%)
  between operations  1.3 us (3%)
    pallas_call x1, Pallas kernels, on_device(): pl.pallas_call(functools.partial(step_kernel, count=count, clusters=clust...  36.4 us
    unnamed x10, local copies, waits for them, and re-layouts  3.27 us

profile of v1, /device:TPU:0, one launch (start us, length us, event | category | flops | bytes accessed | tf_op | source)
XLA Modules:
  0.0 40.9 jit_solution(10415730002487195892)
XLA Ops:
  1.3 36.4 %step_kernel.1 = (f32[3,1536]{1,0:T(4,128)}, f32[3,1536]{1,0:T(4,128)}, f32[3,1536]{1,0:T(4,128)}, f32[1,4]{1,0:T(1,128)}) custom-call(f32[3]{0:T(128)} %box_ref.1, f32[4]{0:T(128)} %extended_ref.1, s32[1]{0:T(128)S(6)} %copy.17.count_ref, f32[3,1536]{1,0:T(4,128)} %position_in.1, f32[3,1536]{1,0:T(4,128)} %velocity_in.1, f32[4,1536]{1,0:T(4,128)} %param_in.1, ...), custom_call_target="tpu_custom_call" | custom-call | tf_op jit(solution)/shard_map/step_kernel/pallas_call | solution.py:401
  37.7 0.0 copy-start.1
  37.7 1.4 %copy.18 = f32[3,1536]{1,0:T(4,128)} copy(f32[3,1536]{1,0:T(4,128)} %get-tuple-element.16) | data formatting | bytes 36864
  39.0 0.0 copy-done.1
  39.0 0.0 copy-start
  39.0 0.6 %copy.19 = f32[3,1536]{1,0:T(4,128)} copy(f32[3,1536]{1,0:T(4,128)S(1)} %copy-done.1) | data formatting | bytes 36864
  39.6 0.1 copy-done
  39.8 0.0 copy-start.2
  39.8 0.6 %copy.20 = f32[3,1536]{1,0:T(4,128)} copy(f32[3,1536]{1,0:T(4,128)S(1)} %copy-done) | data formatting | bytes 36864
  40.4 0.0 copy-done.2
  40.4 0.5 %copy.21 = f32[4]{0:T(128)} copy(f32[4]{0:T(128)S(1)} %bitcast.3) | data formatting | bytes 32
Async XLA Ops:
  37.7 1.4 %copy-start.1 = (f32[3,1536]{1,0:T(4,128)S(1)}, f32[3,1536]{1,0:T(4,128)}, u32[]{:S(2)}) copy-start(f32[3,1536]{1,0:T(4,128)} %get-tuple-element.17) | copy-start | bytes 55300
  39.0 0.7 %copy-start = (f32[3,1536]{1,0:T(4,128)S(1)}, f32[3,1536]{1,0:T(4,128)}, u32[]{:S(2)}) copy-start(f32[3,1536]{1,0:T(4,128)} %get-tuple-element.18) | copy-start | bytes 55300
  39.8 0.7 %copy-start.2 = (f32[1,4]{1,0:T(1,128)S(1)}, f32[1,4]{1,0:T(1,128)}, u32[]{:S(2)}) copy-start(f32[1,4]{1,0:T(1,128)} %get-tuple-element.11) | copy-start | bytes 52

commit v2 on v1

--- a/solution.py
+++ b/solution.py
@@ -15,6 +15,7 @@
 pressure_target = 1.0
 
 LANES = 128
+LANE_BITS = LANES.bit_length() - 1
 FAR_AWAY = 1e36
 
 
@@ -22,16 +23,14 @@
     return (value + unit - 1) // unit * unit
 
 
-def split_two(parts):
-    value = jnp.concatenate(parts, axis=0)
-    high = value.astype(jnp.bfloat16)
-    low = (value - high.astype(jnp.float32)).astype(jnp.bfloat16)
-    return jnp.concatenate([high, low], axis=0)
+def split_two(value):
+    high = value.astype(jnp.bfloat16).astype(jnp.float32)
+    return jnp.concatenate([high, value - high], axis=0).astype(jnp.bfloat16)
 
 
 def picked_rows(table_ref, index, first_tile, last_tile, held=None):
-    within = index & (LANES - 1)
-    block = index // LANES
+    within = (index & (LANES - 1)).astype(jnp.uint32)
+    block = index >> LANE_BITS
     result = []
     for component in range(6):
         value = None if held is None else held[component]
@@ -45,7 +44,7 @@
 
 def step_kernel(
     box_ref, extended_ref, count_ref, position_in, velocity_in, param_in, pair_in, word_in, halo_in,
-    force_out, velocity_out, position_out, coupling_out,
+    folded_out, rate_out,
     position_ref, velocity_ref, param_ref, pair_ref, word_ref, halo_ref,
     table_ref, packed_ref, near_got, far_send, far_got, near_push, far_push, near_back, far_back,
     sum_ref, all_sums, place_ref, folded_ref,
@@ -131,41 +130,39 @@
         copy.wait()
 
     total = count_ref[0]
-    pair_lane = lax.broadcasted_iota(jnp.int32, (16, LANES), 1)
-
-    def hot(column, width, target, at):
-        index = jnp.broadcast_to(column, (LANES, LANES)).astype(jnp.int16)
-        for start in range(0, width, LANES):
-            wanted = (lax.broadcasted_iota(jnp.int32, (LANES, LANES), 1) + start).astype(jnp.int16)
-            target[pl.ds(at, LANES), start : start + LANES] = jnp.where(
-                index == wanted, jnp.bfloat16(1), jnp.bfloat16(0)
+
+    def tile_rows(at, height, row):
+        return pl.ds(pl.multiple_of(at // LANES * height + row, 8), 8)
+
+    ramps = [
+        (lax.broadcasted_iota(jnp.int32, (16, LANES), 0) + group).astype(jnp.float32).astype(jnp.bfloat16)
+        for group in range(0, LANES, 16)
+    ]
+
+    def hot(index, hots, at):
+        low = jnp.broadcast_to((index & (LANES - 1)).astype(jnp.float32), (16, LANES)).astype(jnp.bfloat16)
+        for group in range(LANES // 16):
+            hots[pl.ds(pl.multiple_of(at + group * 16, 16), 16), :] = jnp.where(
+                low == ramps[group], jnp.bfloat16(1), jnp.bfloat16(0)
             )
 
     def prepare(number, carry):
-        rows = []
-        for row in range(2):
-            for part in range(parts):
-                at = pl.multiple_of(number * block + part * LANES, LANES)
-                rows.append(pair_ref[row : row + 1, pl.ds(at, LANES)])
-        if len(rows) % 8:
-            rows.append(jnp.zeros((8 - len(rows) % 8, LANES), jnp.int32))
-        columns = jnp.concatenate(rows, axis=0).T
         for part in range(parts):
             at = pl.multiple_of(number * block + part * LANES, LANES)
             here = pl.ds(at, LANES)
-            hot(columns[:, part : part + 1], first_hot.shape[1], first_hot, at)
-            hot(columns[:, parts + part : parts + part + 1], second_hot.shape[1], second_hot, at)
+            hot(pair_ref[0:1, here], first_hot, at)
+            hot(pair_ref[1:2, here], second_hot, at)
             first = picked_rows(
                 packed_ref, jnp.broadcast_to(pair_ref[0:1, here], (8, LANES)), 0, first_tiles
             )
             for c in range(3):
                 origin = first[c][0:1]
-                first_kept[48 + c : 49 + c, here] = origin
+                first_kept[tile_rows(at, 72, 48 + c * 8), :] = jnp.broadcast_to(origin, (8, LANES))
                 first[c] = first[c] - jnp.broadcast_to(origin, (8, LANES))
             first[4] = 6.0 * first[4]
             first[5] = 12.0 * first[5]
             for c in range(6):
-                first_kept[c * 8 : c * 8 + 8, here] = first[c]
+                first_kept[tile_rows(at, 72, c * 8), :] = first[c]
             words = [jnp.broadcast_to(word_ref[w : w + 1, here], (8, LANES)) for w in range(4)]
             low = jnp.where(sublane < 2, words[0], words[1])
             high = jnp.where(sublane < 6, words[2], words[3])
@@ -173,9 +170,8 @@
             bits = jnp.where(at + lane < total, bits, 0)
             for turn in range(8):
                 wanted = (bits & (1 << ((sublane + turn) & 7))) != 0
-                rows8 = slice(turn * 8, turn * 8 + 8)
-                far_kept[rows8, here] = jnp.where(wanted, 0.0, FAR_AWAY)
-                term_kept[rows8, here] = jnp.where(wanted, reaction_term, 0.0)
+                far_kept[tile_rows(at, 64, turn * 8), :] = jnp.where(wanted, 0.0, FAR_AWAY)
+                term_kept[tile_rows(at, 64, turn * 8), :] = jnp.where(wanted, reaction_term, 0.0)
         return carry
 
     lax.fori_loop(0, blocks, prepare, 0)
@@ -208,10 +204,9 @@
     box_y = box_ref[1]
     box_z = box_ref[2]
 
-    def fetch(number, part):
+    def fetch(number, part, slot):
         at = pl.multiple_of(number * block + part * LANES, LANES)
         here = pl.ds(at, LANES)
-        lanes = slice(part * LANES, (part + 1) * LANES)
         image = jnp.broadcast_to(pair_ref[2:3, here], (8, LANES))
         second = picked_rows(
             table_ref, jnp.broadcast_to(pair_ref[1:2, here], (8, LANES)), 0, second_tiles
@@ -220,31 +215,30 @@
         step_z = image.astype(jnp.float32) - 3.0 * step_y - 4.0
         shift = (None, step_y * box_y, step_z * box_z)
         for c in range(3):
-            second[c] = second[c] - jnp.broadcast_to(first_kept[48 + c : 49 + c, here], (8, LANES))
+            second[c] = second[c] - first_kept[tile_rows(at, 72, 48 + c * 8), :]
             if shift[c] is not None:
                 second[c] = second[c] + shift[c]
         for c in range(6):
-            second_got[c * 8 : c * 8 + 8, lanes] = second[c]
+            low = slot * 96 + c * 16
+            second_got[low : low + 8, :] = second[c]
+            second_got[low + 8 : low + 16, :] = second[c]
 
     def interact(number, part):
-        here = pl.ds(pl.multiple_of(number * block + part * LANES, LANES), LANES)
-        lanes = slice(part * LANES, (part + 1) * LANES)
-        first = [first_kept[c * 8 : c * 8 + 8, here] for c in range(6)]
-        second = [second_got[c * 8 : c * 8 + 8, lanes] for c in range(6)]
+        at = pl.multiple_of(number * block + part * LANES, LANES)
+        first = [first_kept[tile_rows(at, 72, c * 8), :] for c in range(6)]
+        low = (part % 2) * 96
         charge, dispersion, repulsion = first[3], first[4], first[5]
-        moving = second
         from_first = [None] * 3
         onto_second = [None] * 3
         for turn in range(7, -1, -1):
-            moving = [pltpu.roll(m, 1, 0) for m in moving] if turn else second
+            moving = [second_got[low + c * 16 + turn : low + c * 16 + turn + 8, :] for c in range(6)]
             delta = [moving[c] - first[c] for c in range(3)]
-            rows8 = slice(turn * 8, turn * 8 + 8)
             radius_sq = delta[0] * delta[0] + delta[1] * delta[1] + delta[2] * delta[2]
-            inverse = lax.rsqrt(radius_sq + far_kept[rows8, here])
+            inverse = lax.rsqrt(radius_sq + far_kept[tile_rows(at, 64, turn * 8), :])
             inverse_sq = inverse * inverse
             cube = inverse * inverse_sq
             six = cube * cube
-            scalar = charge * moving[3] * (cube - term_kept[rows8, here]) + (
+            scalar = charge * moving[3] * (cube - term_kept[tile_rows(at, 64, turn * 8), :]) + (
                 repulsion * moving[5] * six - dispersion * moving[4]
             ) * (six * inverse_sq)
             for c in range(3):
@@ -255,43 +249,58 @@
                 else:
                     from_first[c] = from_first[c] + force
                     onto_second[c] = pltpu.roll(onto_second[c], 1, 0) + force
-        first_terms[:, lanes] = split_two(from_first)
-        second_terms[:, lanes] = split_two(onto_second)
-        return [onto_second[c] * second[c] - from_first[c] * first[c] for c in range(3)]
+        for c in range(3):
+            first_terms[part * 24 + c * 8 : part * 24 + c * 8 + 8, :] = from_first[c]
+            second_terms[part * 24 + c * 8 : part * 24 + c * 8 + 8, :] = onto_second[c]
+        return [onto_second[c] * moving[c] - from_first[c] * first[c] for c in range(3)]
 
     def spread(number):
-        here = pl.ds(pl.multiple_of(number * block, LANES), block)
-        contract = (((1,), (0,)), ((), ()))
-        own_ref[...] += lax.dot_general(
-            first_terms[...], first_hot[here, :], contract, preferred_element_type=jnp.float32
-        )
-        other_ref[...] += lax.dot_general(
-            second_terms[...], second_hot[here, :], contract, preferred_element_type=jnp.float32
-        )
-
-    for part in range(parts):
-        fetch(0, part)
+        for target, terms, row, hots, tiles in (
+            (own_ref, first_terms, 0, first_hot, first_tiles),
+            (other_ref, second_terms, 1, second_hot, second_tiles),
+        ):
+            rows = []
+            columns = []
+            for part in range(parts):
+                at = pl.multiple_of(number * block + part * LANES, LANES)
+                home = jnp.broadcast_to(pair_ref[row : row + 1, pl.ds(at, LANES)] >> LANE_BITS, (16, LANES))
+                home = home.astype(jnp.float32).astype(jnp.bfloat16)
+                home = jnp.concatenate([home] * 3, axis=0)
+                pieces = split_two(terms[part * 24 : part * 24 + 24, :])
+                rows.append(jnp.concatenate([
+                    jnp.where(home == jnp.bfloat16(tile), pieces, jnp.bfloat16(0)) for tile in range(tiles)
+                ], axis=0))
+                columns.append(hots[pl.ds(at, LANES), :])
+            target[...] += lax.dot_general(
+                jnp.concatenate(rows, axis=1), jnp.concatenate(columns, axis=1),
+                (((1,), (1,)), ((), ())), preferred_element_type=jnp.float32,
+            )
+
+    fetch(0, 0, 0)
 
     def one_block(number, carry):
         spread(jnp.maximum(number - 1, 0))
         upcoming = jnp.minimum(number + 1, blocks - 1)
         virial = [virial_ref[c * 8 : c * 8 + 8, :] for c in range(3)]
         for part in range(parts):
+            if part + 1 < parts:
+                fetch(number, part + 1, (part + 1) % 2)
+            else:
+                fetch(upcoming, 0, 0)
             added = interact(number, part)
             virial = [virial[c] + added[c] for c in range(3)]
-            fetch(upcoming, part)
         for c in range(3):
             virial_ref[c * 8 : c * 8 + 8, :] = virial[c]
         return carry
 
     lax.fori_loop(0, blocks, one_block, 0)
+    row = jnp.zeros((1, LANES), jnp.float32)
+    for c in range(3):
+        added = jnp.sum(virial_ref[c * 8 : c * 8 + 8, :], axis=0, keepdims=True)
+        row = jnp.where(lane[0:1] == c, jnp.sum(added, axis=1, keepdims=True) * -0.5, row)
+        row = jnp.where(lane[0:1] == c + 3, energy[c : c + 1], row)
+    sum_ref[...] = row
     spread(blocks - 1)
-    rows = [
-        jnp.sum(jnp.sum(virial_ref[c * 8 : c * 8 + 8, :], axis=0, keepdims=True), axis=1, keepdims=True) * -0.5
-        for c in range(3)
-    ]
-    rows = rows + [energy, jnp.zeros((2, 1), jnp.float32)]
-    sum_ref[...] = jnp.broadcast_to(jnp.concatenate(rows, axis=0), (8, LANES))
 
     def sum_copy(step, source):
         return pltpu.make_async_remote_copy(
@@ -308,24 +317,29 @@
         sum_copy(step, lax.rem(me + count - step, count)).wait()
         return carry
 
-    other = other_ref[0:24, :] + other_ref[24:48, :]
+    def joined(ref, tiles):
+        return jnp.concatenate([
+            ref[tile * 48 : tile * 48 + 24, :] + ref[tile * 48 + 24 : tile * 48 + 48, :]
+            for tile in range(tiles)
+        ], axis=1)
+
+    other = joined(other_ref, second_tiles)
+    own = joined(own_ref, first_tiles)
     near_push[:, 0:clusters] = other[:, clusters : 2 * clusters]
     far_push[:, 0:far_count] = other[:, 2 * clusters : slots]
+    lax.fori_loop(1, count, give, 0)
     homeward = [remote(far_push, far_back, 3, 2), remote(near_push, near_back, 2, 1)]
     for copy in homeward:
         copy.start()
-    lax.fori_loop(1, count, give, 0)
     all_sums[me] = sum_ref[...]
-    folded_ref[:, 0:clusters] = (
-        other[:, 0:clusters] - own_ref[0:24, 0:clusters] - own_ref[24:48, 0:clusters]
-    )
+    folded_ref[:, 0:clusters] = other[:, 0:clusters] - own[:, 0:clusters]
     for copy in homeward:
         copy.wait()
     place = place_ref[...]
     for base in range(0, clusters, LANES):
         lanes = slice(base, base + LANES)
         index = place[:, lanes]
-        within = jnp.maximum(index, 0) & (LANES - 1)
+        within = (jnp.maximum(index, 0) & (LANES - 1)).astype(jnp.uint32)
         for c in range(3):
             rows8 = slice(c * 8, c * 8 + 8)
             value = folded_ref[rows8, lanes] + near_back[rows8, lanes]
@@ -334,39 +348,47 @@
                 picked = jnp.take_along_axis(source, within, axis=1, mode="promise_in_bounds")
                 mine = (index >= tile * LANES) & (index < (tile + 1) * LANES)
                 value = value + jnp.where(mine, picked, 0.0)
-            folded_ref[rows8, lanes] = value
+            folded_out[rows8, lanes] = value
+    lax.fori_loop(1, count, take, 0)
+    totals = lax.fori_loop(
+        0, count, lambda source, held: held + all_sums[source], jnp.zeros((1, LANES), jnp.float32)
+    )
+    virial = [jnp.broadcast_to(totals[:, c : c + 1], (1, LANES)) for c in range(3)]
+    kinetic = [jnp.broadcast_to(totals[:, c : c + 1], (1, LANES)) for c in range(3, 6)]
+    energy = kinetic[0] + kinetic[1] + kinetic[2]
+    volume = box_ref[0] * box_ref[1] * box_ref[2]
+    ratio = 2.0 * energy / (3.0 * count * clusters * 8 * thermal_scale_unit)
+    rate_out[3:4] = extended_ref[0] + reservoir_inertia_mass * (ratio - 1.0)
+    for c in range(3):
+        change = barostat_gain * (kinetic[c] - virial[c] - pressure_target * volume / 2.0) / (energy / 3.0)
+        rate_out[c : c + 1] = extended_ref[1 + c] + change
+
+
+def final_kernel(
+    folded_ref, rate_ref, position_ref, velocity_ref, param_ref,
+    force_out, velocity_out, position_out, coupling_out, *, clusters
+):
+    sublane = lax.broadcasted_iota(jnp.int32, (8, LANES), 0)
+    lane = lax.broadcasted_iota(jnp.int32, (8, LANES), 1)
     wanted = sublane == (lane & 7)
     for c in range(3):
         for tile in range(clusters * 8 // LANES):
             at = tile * 16
             source = folded_ref[c * 8 : c * 8 + 8, at // LANES * LANES : at // LANES * LANES + LANES]
-            picked = jnp.take_along_axis(
-                source, at % LANES + lane // 8, axis=1, mode="promise_in_bounds"
-            )
+            index = (at % LANES + lane // 8).astype(jnp.uint32)
+            picked = jnp.take_along_axis(source, index, axis=1, mode="promise_in_bounds")
             force_out[c : c + 1, tile * LANES : (tile + 1) * LANES] = jnp.sum(
                 jnp.where(wanted, picked, 0.0), axis=0, keepdims=True
             )
-    lax.fori_loop(1, count, take, 0)
-    totals = lax.fori_loop(
-        0, count, lambda source, held: held + all_sums[source], jnp.zeros((8, LANES), jnp.float32)
-    )
-    virial = totals[0:3]
-    kinetic = totals[3:6]
-    energy = totals[3:4] + totals[4:5] + totals[5:6]
-    volume = box_ref[0] * box_ref[1] * box_ref[2]
-    ratio = 2.0 * energy / (3.0 * count * clusters * 8 * thermal_scale_unit)
-    damping = extended_ref[0] + reservoir_inertia_mass * (ratio - 1.0)
-    change = barostat_gain * (kinetic - virial - pressure_target * volume / 2.0) / (energy / 3.0)
-    row = damping
-    rates = []
+    row = rate_ref[3:4, :]
     for c in range(3):
-        rates.append(extended_ref[1 + c] + change[c : c + 1])
-        row = jnp.where(lane[0:1] == c + 1, rates[c], row)
+        row = jnp.where(lane[0:1] == c + 1, rate_ref[c : c + 1, :], row)
     coupling_out[...] = row[:, 0:4]
-    rates = jnp.concatenate(rates, axis=0)[:, 0:1]
+    rates = rate_ref[0:3, 0:1]
+    damping = rate_ref[3:4, 0:1]
     velocity = velocity_ref[...]
     moved = velocity + time_step * (
-        force_out[...] * param_ref[3:4, :] - (damping[:, 0:1] + rates) * velocity
+        force_out[...] * param_ref[3:4, :] - (damping + rates) * velocity
     )
     velocity_out[...] = moved
     position_out[...] = position_ref[...] * (1.0 + time_step * rates) + time_step * moved
@@ -388,7 +410,7 @@
     slots = 2 * clusters + far_clusters
     pairs = pair_list.shape[1]
     count = lax.axis_size("gx")
-    block = next(b for b in (512, 384, 256, 128) if pairs % b == 0)
+    block = next(b for b in (768, 512, 384, 256, 128) if pairs % b == 0)
     wide = round_up(clusters, LANES)
     wide_far = round_up(far_clusters, LANES)
     wide_slots = round_up(slots, LANES)
@@ -398,24 +420,26 @@
     shape = jax.ShapeDtypeStruct(positions.shape, jnp.float32)
     f32 = lambda *dims: pltpu.VMEM(dims, jnp.float32)
     halo = halo_far[None, :]
-    forces, new_velocities, new_positions, new_coupling = pl.pallas_call(
+    folded, rates = pl.pallas_call(
         functools.partial(step_kernel, count=count, clusters=clusters, slots=slots, block=block),
         name="step_kernel",
-        out_shape=(shape,) * 3 + (jax.ShapeDtypeStruct((1, 4), jnp.float32),),
+        out_shape=(
+            jax.ShapeDtypeStruct((24, wide), jnp.float32), jax.ShapeDtypeStruct((4, LANES), jnp.float32)
+        ),
         in_specs=[smem] * 3 + [anywhere] * 6,
-        out_specs=(vmem,) * 4,
+        out_specs=(vmem,) * 2,
         scratch_shapes=[
             f32(*positions.shape), f32(*velocities.shape), f32(*atom_params.shape),
             pltpu.VMEM(pair_list.shape, jnp.int32), pltpu.VMEM(exclusion.shape, jnp.int32),
             pltpu.VMEM(halo.shape, jnp.int32),
             f32(48, wide_slots), f32(48, wide), f32(48, wide), f32(48, wide_far), f32(48, wide_far),
             f32(24, wide), f32(24, wide_far), f32(24, wide), f32(24, wide_far),
-            f32(8, LANES), f32(count, 8, LANES),
+            f32(1, LANES), f32(count, 1, LANES),
             pltpu.VMEM((8, wide), jnp.int32), f32(24, wide),
-            f32(56, pairs), f32(64, pairs), f32(64, pairs),
-            pltpu.VMEM((pairs, wide), jnp.bfloat16), pltpu.VMEM((pairs, wide_slots), jnp.bfloat16),
-            f32(48, block), pltpu.VMEM((48, block), jnp.bfloat16), pltpu.VMEM((48, block), jnp.bfloat16),
-            f32(48, wide), f32(48, wide_slots), f32(24, LANES),
+            f32(pairs // LANES * 72, LANES), f32(pairs // LANES * 64, LANES), f32(pairs // LANES * 64, LANES),
+pltpu.VMEM((pairs, LANES), jnp.bfloat16), pltpu.VMEM((pairs, LANES), jnp.bfloat16),
+            f32(192, LANES), f32(block // LANES * 24, LANES), f32(block // LANES * 24, LANES),
+            f32(wide // LANES * 48, LANES), f32(wide_slots // LANES * 48, LANES), f32(24, LANES),
             pltpu.SemaphoreType.DMA((6,)), pltpu.SemaphoreType.DMA((4,)), pltpu.SemaphoreType.DMA((4,)),
             pltpu.SemaphoreType.DMA((count,)), pltpu.SemaphoreType.DMA((count,)),
         ],
@@ -423,6 +447,13 @@
             collective_id=0, has_side_effects=True, vmem_limit_bytes=60 * 1024 * 1024
         ),
     )(box_lengths, extended_variables, pair_count, positions, velocities, atom_params, pair_list, exclusion, halo)
+    forces, new_velocities, new_positions, new_coupling = pl.pallas_call(
+        functools.partial(final_kernel, clusters=clusters),
+        name="final_kernel",
+        out_shape=(shape,) * 3 + (jax.ShapeDtypeStruct((1, 4), jnp.float32),),
+        in_specs=[vmem] * 5,
+        out_specs=(vmem,) * 4,
+    )(folded, rates, positions, velocities, atom_params)
     return (forces, new_velocities, new_positions, new_coupling.reshape(4))
 
 

time: 41.2 us -> 30.2 us (0.73)
  Pallas kernels: 36.4 us -> 28.7 us
  local copies, waits for them, and re-layouts: 3.27 us -> 0 us
    pallas_call x1, Pallas kernels: 36.4 us -> 27.1 us  [on_device(): pl.pallas_call(functools.partial(step_kernel, count=count, clusters=clust...]
    unnamed x10 -> x0, local copies, waits for them, and re-layouts: 3.27 us -> none
    pallas_call x0 -> x1, Pallas kernels: none -> 1.61 us  [on_device(): pl.pallas_call(functools.partial(final_kernel, clusters=clusters), name='...]
where the time goes in v2:
time: 30.2 us; the launch traced here: 30 us
  Pallas kernels  28.7 us (95%)
  between operations  1.29 us (4%)
    pallas_call x1, Pallas kernels, on_device(): pl.pallas_call(functools.partial(step_kernel, count=count, clusters=clust...  27.1 us
    pallas_call x1, Pallas kernels, on_device(): pl.pallas_call(functools.partial(final_kernel, clusters=clusters), name='...  1.61 us

profile of v2, /device:TPU:0, one launch (start us, length us, event | category | flops | bytes accessed | tf_op | source)
XLA Modules:
  0.0 30.0 jit_solution(4051315467872855682)
XLA Ops:
  1.3 27.1 %step_kernel.1 = (f32[24,256]{1,0:T(8,128)}, f32[4,128]{1,0:T(4,128)}) custom-call(f32[3]{0:T(128)} %box_ref.1, f32[4]{0:T(128)} %extended_ref.1, s32[1]{0:T(128)S(6)} %copy.13.count_ref, f32[3,1536]{1,0:T(4,128)} %position_ref.1, f32[3,1536]{1,0:T(4,128)} %velocity_ref.1, f32[4,1536]{1,0:T(4,128)} %param_ref.1, s32[3,16896]{1,0:T(4,128)} %pair_in.1, ...), custom_call_target="tpu_custom_call" | custom-call | tf_op jit(solution)/shard_map/step_kernel/pallas_call | solution.py:423
  28.4 1.6 %final_kernel.1 = (f32[3,1536]{1,0:T(4,128)}, f32[3,1536]{1,0:T(4,128)}, f32[3,1536]{1,0:T(4,128)}, f32[1,4]{1,0:T(1,128)}) custom-call(f32[24,256]{1,0:T(8,128)} %get-tuple-element.10.folded_ref, f32[4,128]{1,0:T(4,128)} %get-tuple-element.11.rate_ref, f32[3,1536]{1,0:T(4,128)} %position_ref.1, f32[3,1536]{1,0:T(4,128)} %velocity_ref.1, f32[4,1536]{1,0:T(4,128)} %param_ref.1), custom_call_target="tpu_custom_call" | custom-call | tf_op jit(solution)/shard_map/final_kernel/pallas_call | solution.py:450

commit v3 on v2

--- a/solution.py
+++ b/solution.py
@@ -43,8 +43,8 @@
 
 
 def step_kernel(
-    box_ref, extended_ref, count_ref, position_in, velocity_in, param_in, pair_in, word_in, halo_in,
-    folded_out, rate_out,
+    box_in, extended_in, count_in, position_in, velocity_in, param_in, pair_in, word_in, halo_in,
+    folded_out, rate_out, box_ref, extended_ref, count_ref,
     position_ref, velocity_ref, param_ref, pair_ref, word_ref, halo_ref,
     table_ref, packed_ref, near_got, far_send, far_got, near_push, far_push, near_back, far_back,
     sum_ref, all_sums, place_ref, folded_ref,
@@ -69,12 +69,16 @@
         )
         return carry
 
-    lax.fori_loop(1, count, greet, 0)
+    close = sorted({1, count - 1, 2, count - 2} - {0, count})
+    for step in close:
+        greet(step, 0)
+    lax.fori_loop(3, count - 2, greet, 0)
     inward = [
         pltpu.make_async_copy(source, target, local_sems.at[number])
         for number, (source, target) in enumerate((
             (position_in, position_ref), (param_in, param_ref), (halo_in, halo_ref),
-            (pair_in, pair_ref), (word_in, word_ref), (velocity_in, velocity_ref),
+            (pair_in, pair_ref), (word_in, word_ref), (count_in, count_ref), (box_in, box_ref),
+            (velocity_in, velocity_ref), (extended_in, extended_ref),
         ))
     ]
     for copy in inward:
@@ -126,10 +130,12 @@
     outward = [remote(far_send, far_got, 1, count - 2), remote(packed_ref, near_got, 0, count - 1)]
     for copy in outward:
         copy.start()
-    for copy in inward[3:]:
+    for copy in inward[3:7]:
         copy.wait()
 
     total = count_ref[0]
+    box_y = box_ref[1]
+    box_z = box_ref[2]
 
     def tile_rows(at, height, row):
         return pl.ds(pl.multiple_of(at // LANES * height + row, 8), 8)
@@ -157,12 +163,17 @@
             )
             for c in range(3):
                 origin = first[c][0:1]
-                first_kept[tile_rows(at, 72, 48 + c * 8), :] = jnp.broadcast_to(origin, (8, LANES))
+                first_kept[tile_rows(at, 88, 48 + c * 8), :] = jnp.broadcast_to(origin, (8, LANES))
                 first[c] = first[c] - jnp.broadcast_to(origin, (8, LANES))
             first[4] = 6.0 * first[4]
             first[5] = 12.0 * first[5]
             for c in range(6):
-                first_kept[tile_rows(at, 72, c * 8), :] = first[c]
+                first_kept[tile_rows(at, 88, c * 8), :] = first[c]
+            image = jnp.broadcast_to(pair_ref[2:3, here], (8, LANES))
+            step_y = jnp.where(image >= 6, 1.0, jnp.where(image >= 3, 0.0, -1.0))
+            step_z = image.astype(jnp.float32) - 3.0 * step_y - 4.0
+            first_kept[tile_rows(at, 88, 72), :] = step_y * box_y
+            first_kept[tile_rows(at, 88, 80), :] = step_z * box_z
             words = [jnp.broadcast_to(word_ref[w : w + 1, here], (8, LANES)) for w in range(4)]
             low = jnp.where(sublane < 2, words[0], words[1])
             high = jnp.where(sublane < 6, words[2], words[3])
@@ -175,6 +186,8 @@
         return carry
 
     lax.fori_loop(0, blocks, prepare, 0)
+    for copy in inward[7:]:
+        copy.wait()
     energy = velocity_ref[...] * velocity_ref[...] / param_ref[3:4, :]
     energy = 0.5 * jnp.sum(energy, axis=1, keepdims=True)
     place_ref[...] = jnp.full_like(place_ref, -1)
@@ -201,37 +214,31 @@
     table_ref[:, clusters : 2 * clusters] = near_got[:, 0:clusters] + jnp.where(upper, near_lift, 0.0)
     upper = lax.broadcasted_iota(jnp.int32, (48, far_count), 0) < 8
     table_ref[:, 2 * clusters : slots] = far_got[:, 0:far_count] + jnp.where(upper, far_lift, 0.0)
-    box_y = box_ref[1]
-    box_z = box_ref[2]
 
     def fetch(number, part, slot):
         at = pl.multiple_of(number * block + part * LANES, LANES)
         here = pl.ds(at, LANES)
-        image = jnp.broadcast_to(pair_ref[2:3, here], (8, LANES))
         second = picked_rows(
             table_ref, jnp.broadcast_to(pair_ref[1:2, here], (8, LANES)), 0, second_tiles
         )
-        step_y = jnp.where(image >= 6, 1.0, jnp.where(image >= 3, 0.0, -1.0))
-        step_z = image.astype(jnp.float32) - 3.0 * step_y - 4.0
-        shift = (None, step_y * box_y, step_z * box_z)
         for c in range(3):
-            second[c] = second[c] - first_kept[tile_rows(at, 72, 48 + c * 8), :]
-            if shift[c] is not None:
-                second[c] = second[c] + shift[c]
+            second[c] = second[c] - first_kept[tile_rows(at, 88, 48 + c * 8), :]
+            if c:
+                second[c] = second[c] + first_kept[tile_rows(at, 88, 64 + c * 8), :]
         for c in range(6):
-            low = slot * 96 + c * 16
-            second_got[low : low + 8, :] = second[c]
-            second_got[low + 8 : low + 16, :] = second[c]
+            second_got[slot * 48 + c * 8 : slot * 48 + c * 8 + 8, :] = second[c]
 
     def interact(number, part):
         at = pl.multiple_of(number * block + part * LANES, LANES)
-        first = [first_kept[tile_rows(at, 72, c * 8), :] for c in range(6)]
-        low = (part % 2) * 96
+        first = [first_kept[tile_rows(at, 88, c * 8), :] for c in range(6)]
+        low = (part % 2) * 48
         charge, dispersion, repulsion = first[3], first[4], first[5]
         from_first = [None] * 3
         onto_second = [None] * 3
         for turn in range(7, -1, -1):
-            moving = [second_got[low + c * 16 + turn : low + c * 16 + turn + 8, :] for c in range(6)]
+            moving = [second_got[low + c * 8 : low + c * 8 + 8, :] for c in range(6)]
+            if turn:
+                moving = [pltpu.roll(m, 8 - turn, 0) for m in moving]
             delta = [moving[c] - first[c] for c in range(3)]
             radius_sq = delta[0] * delta[0] + delta[1] * delta[1] + delta[2] * delta[2]
             inverse = lax.rsqrt(radius_sq + far_kept[tile_rows(at, 64, turn * 8), :])
@@ -327,10 +334,10 @@
     own = joined(own_ref, first_tiles)
     near_push[:, 0:clusters] = other[:, clusters : 2 * clusters]
     far_push[:, 0:far_count] = other[:, 2 * clusters : slots]
-    lax.fori_loop(1, count, give, 0)
     homeward = [remote(far_push, far_back, 3, 2), remote(near_push, near_back, 2, 1)]
     for copy in homeward:
         copy.start()
+    lax.fori_loop(1, count, give, 0)
     all_sums[me] = sum_ref[...]
     folded_ref[:, 0:clusters] = other[:, 0:clusters] - own[:, 0:clusters]
     for copy in homeward:
@@ -415,7 +422,6 @@
     wide_far = round_up(far_clusters, LANES)
     wide_slots = round_up(slots, LANES)
     vmem = pl.BlockSpec(memory_space=pltpu.VMEM)
-    smem = pl.BlockSpec(memory_space=pltpu.SMEM)
     anywhere = pl.BlockSpec(memory_space=pl.ANY)
     shape = jax.ShapeDtypeStruct(positions.shape, jnp.float32)
     f32 = lambda *dims: pltpu.VMEM(dims, jnp.float32)
@@ -426,9 +432,11 @@
         out_shape=(
             jax.ShapeDtypeStruct((24, wide), jnp.float32), jax.ShapeDtypeStruct((4, LANES), jnp.float32)
         ),
-        in_specs=[smem] * 3 + [anywhere] * 6,
+        in_specs=[anywhere] * 9,
         out_specs=(vmem,) * 2,
         scratch_shapes=[
+            pltpu.SMEM(box_lengths.shape, jnp.float32), pltpu.SMEM(extended_variables.shape, jnp.float32),
+            pltpu.SMEM(pair_count.shape, jnp.int32),
             f32(*positions.shape), f32(*velocities.shape), f32(*atom_params.shape),
             pltpu.VMEM(pair_list.shape, jnp.int32), pltpu.VMEM(exclusion.shape, jnp.int32),
             pltpu.VMEM(halo.shape, jnp.int32),
@@ -436,11 +444,11 @@
             f32(24, wide), f32(24, wide_far), f32(24, wide), f32(24, wide_far),
             f32(1, LANES), f32(count, 1, LANES),
             pltpu.VMEM((8, wide), jnp.int32), f32(24, wide),
-            f32(pairs // LANES * 72, LANES), f32(pairs // LANES * 64, LANES), f32(pairs // LANES * 64, LANES),
+            f32(pairs // LANES * 88, LANES), f32(pairs // LANES * 64, LANES), f32(pairs // LANES * 64, LANES),
 pltpu.VMEM((pairs, LANES), jnp.bfloat16), pltpu.VMEM((pairs, LANES), jnp.bfloat16),
-            f32(192, LANES), f32(block // LANES * 24, LANES), f32(block // LANES * 24, LANES),
+            f32(96, LANES), f32(block // LANES * 24, LANES), f32(block // LANES * 24, LANES),
             f32(wide // LANES * 48, LANES), f32(wide_slots // LANES * 48, LANES), f32(24, LANES),
-            pltpu.SemaphoreType.DMA((6,)), pltpu.SemaphoreType.DMA((4,)), pltpu.SemaphoreType.DMA((4,)),
+            pltpu.SemaphoreType.DMA((9,)), pltpu.SemaphoreType.DMA((4,)), pltpu.SemaphoreType.DMA((4,)),
             pltpu.SemaphoreType.DMA((count,)), pltpu.SemaphoreType.DMA((count,)),
         ],
         compiler_params=pltpu.CompilerParams(

time: 30.2 us -> 28.6 us (0.947)
  Pallas kernels: 28.7 us -> 27.1 us
    pallas_call x1, Pallas kernels: 27.1 us -> 25.5 us  [on_device(): pl.pallas_call(functools.partial(step_kernel, count=count, clusters=clust...]
where the time goes in v3:
time: 28.6 us; the launch traced here: 28.4 us
  Pallas kernels  27.1 us (95%)
  between operations  1.29 us (5%)
    pallas_call x1, Pallas kernels, on_device(): pl.pallas_call(functools.partial(step_kernel, count=count, clusters=clust...  25.5 us
    pallas_call x1, Pallas kernels, on_device(): pl.pallas_call(functools.partial(final_kernel, clusters=clusters), name='...  1.61 us

profile of v3, /device:TPU:0, one launch (start us, length us, event | category | flops | bytes accessed | tf_op | source)
XLA Modules:
  0.0 28.4 jit_solution(5632288017000633804)
XLA Ops:
  1.3 25.5 %step_kernel.1 = (f32[24,256]{1,0:T(8,128)}, f32[4,128]{1,0:T(4,128)}) custom-call(f32[3]{0:T(128)} %box_in.1, f32[4]{0:T(128)} %extended_in.1, s32[1]{0:T(128)S(6)} %copy.13.count_in, f32[3,1536]{1,0:T(4,128)} %position_ref.1, f32[3,1536]{1,0:T(4,128)} %velocity_ref.1, f32[4,1536]{1,0:T(4,128)} %param_ref.1, s32[3,16896]{1,0:T(4,128)} %pair_in.1, ...), custom_call_target="tpu_custom_call" | custom-call | tf_op jit(solution)/shard_map/step_kernel/pallas_call | solution.py:429
  26.8 1.6 %final_kernel.1 = (f32[3,1536]{1,0:T(4,128)}, f32[3,1536]{1,0:T(4,128)}, f32[3,1536]{1,0:T(4,128)}, f32[1,4]{1,0:T(1,128)}) custom-call(f32[24,256]{1,0:T(8,128)} %get-tuple-element.10.folded_ref, f32[4,128]{1,0:T(4,128)} %get-tuple-element.11.rate_ref, f32[3,1536]{1,0:T(4,128)} %position_ref.1, f32[3,1536]{1,0:T(4,128)} %velocity_ref.1, f32[4,1536]{1,0:T(4,128)} %param_ref.1), custom_call_target="tpu_custom_call" | custom-call | tf_op jit(solution)/shard_map/final_kernel/pallas_call | solution.py:458

commit v4 on v3

--- a/solution.py
+++ b/solution.py
@@ -422,17 +422,17 @@
     wide_far = round_up(far_clusters, LANES)
     wide_slots = round_up(slots, LANES)
     vmem = pl.BlockSpec(memory_space=pltpu.VMEM)
-    anywhere = pl.BlockSpec(memory_space=pl.ANY)
     shape = jax.ShapeDtypeStruct(positions.shape, jnp.float32)
     f32 = lambda *dims: pltpu.VMEM(dims, jnp.float32)
     halo = halo_far[None, :]
+    pinned = lambda array: pltpu.with_memory_space_constraint(array, pltpu.HBM)
     folded, rates = pl.pallas_call(
         functools.partial(step_kernel, count=count, clusters=clusters, slots=slots, block=block),
         name="step_kernel",
         out_shape=(
             jax.ShapeDtypeStruct((24, wide), jnp.float32), jax.ShapeDtypeStruct((4, LANES), jnp.float32)
         ),
-        in_specs=[anywhere] * 9,
+        in_specs=[pl.BlockSpec(memory_space=pltpu.HBM)] * 9,
         out_specs=(vmem,) * 2,
         scratch_shapes=[
             pltpu.SMEM(box_lengths.shape, jnp.float32), pltpu.SMEM(extended_variables.shape, jnp.float32),
@@ -452,15 +452,19 @@
             pltpu.SemaphoreType.DMA((count,)), pltpu.SemaphoreType.DMA((count,)),
         ],
         compiler_params=pltpu.CompilerParams(
-            collective_id=0, has_side_effects=True, vmem_limit_bytes=60 * 1024 * 1024
+            collective_id=0, has_side_effects=True, vmem_limit_bytes=32 * 1024 * 1024
         ),
-    )(box_lengths, extended_variables, pair_count, positions, velocities, atom_params, pair_list, exclusion, halo)
+    )(
+        pinned(box_lengths), pinned(extended_variables), pair_count, pinned(positions), pinned(velocities),
+        pinned(atom_params), pinned(pair_list), pinned(exclusion), pinned(halo),
+    )
     forces, new_velocities, new_positions, new_coupling = pl.pallas_call(
         functools.partial(final_kernel, clusters=clusters),
         name="final_kernel",
         out_shape=(shape,) * 3 + (jax.ShapeDtypeStruct((1, 4), jnp.float32),),
         in_specs=[vmem] * 5,
         out_specs=(vmem,) * 4,
+        compiler_params=pltpu.CompilerParams(vmem_limit_bytes=4 * 1024 * 1024),
     )(folded, rates, positions, velocities, atom_params)
     return (forces, new_velocities, new_positions, new_coupling.reshape(4))
 

time: 28.6 us -> 27.2 us (0.951)
  Pallas kernels: 27.1 us -> 25.6 us
    pallas_call x1, Pallas kernels: 1.61 us -> 0.81 us  [on_device(): pl.pallas_call(functools.partial(final_kernel, clusters=clusters), name='...]
    pallas_call x1, Pallas kernels: 25.5 us -> 24.8 us  [on_device(): pl.pallas_call(functools.partial(step_kernel, count=count, clusters=clust...]
where the time goes in v4:
time: 27.2 us; the launch traced here: 27 us
  Pallas kernels  25.6 us (94%)
  between operations  1.33 us (5%)
    pallas_call x1, Pallas kernels, on_device(): pl.pallas_call(functools.partial(step_kernel, count=count, clusters=clust...  24.8 us
    pallas_call x1, Pallas kernels, on_device(): pl.pallas_call(functools.partial(final_kernel, clusters=clusters), name='...  0.81 us

profile of v4, /device:TPU:0, one launch (start us, length us, event | category | flops | bytes accessed | tf_op | source)
XLA Modules:
  0.0 27.0 jit_solution(3905572356994482800)
XLA Ops:
  1.3 0.0 copy-start
  1.3 0.0 copy-start.1
  1.3 0.0 copy-start.2
  1.3 24.8 %step_kernel.1 = (f32[24,256]{1,0:T(8,128)S(1)}, f32[4,128]{1,0:T(4,128)S(1)}) custom-call(f32[3]{0:T(128)} %box_in.1, f32[4]{0:T(128)} %extended_in.1, s32[1]{0:T(128)S(6)} %copy.13.count_in, f32[3,1536]{1,0:T(4,128)} %position_ref.1, f32[3,1536]{1,0:T(4,128)} %velocity_ref.1, f32[4,1536]{1,0:T(4,128)} %param_ref.1, s32[3,16896]{1,0:T(4,128)} %pair_in.1, ...), custom_call_target="tpu_custom_call" | custom-call | tf_op jit(solution)/shard_map/step_kernel/pallas_call | solution.py:429
  26.2 0.0 copy-done
  26.2 0.0 copy-done.1
  26.2 0.0 copy-done.2
  26.2 0.8 %final_kernel.1 = (f32[3,1536]{1,0:T(4,128)}, f32[3,1536]{1,0:T(4,128)}, f32[3,1536]{1,0:T(4,128)}, f32[1,4]{1,0:T(1,128)}) custom-call(f32[24,256]{1,0:T(8,128)S(1)} %get-tuple-element.10.folded_ref, f32[4,128]{1,0:T(4,128)S(1)} %get-tuple-element.11.rate_ref, f32[3,1536]{1,0:T(4,128)S(1)} %copy-done, f32[3,1536]{1,0:T(4,128)S(1)} %copy-done.1, ...), custom_call_target="tpu_custom_call" | custom-call | tf_op jit(solution)/shard_map/final_kernel/pallas_call | solution.py:461
Async XLA Ops:
  1.3 24.9 %copy-start = (f32[3,1536]{1,0:T(4,128)S(1)}, f32[3,1536]{1,0:T(4,128)}, u32[]{:S(2)}) copy-start(f32[3,1536]{1,0:T(4,128)} %position_ref.1) | copy-start | bytes 55300
  1.3 24.9 %copy-start.1 = (f32[3,1536]{1,0:T(4,128)S(1)}, f32[3,1536]{1,0:T(4,128)}, u32[]{:S(2)}) copy-start(f32[3,1536]{1,0:T(4,128)} %velocity_ref.1) | copy-start | bytes 55300
  1.3 24.9 %copy-start.2 = (f32[4,1536]{1,0:T(4,128)S(1)}, f32[4,1536]{1,0:T(4,128)}, u32[]{:S(2)}) copy-start(f32[4,1536]{1,0:T(4,128)} %param_ref.1) | copy-start | bytes 73732

commit v5 on v4

--- a/solution.py
+++ b/solution.py
@@ -21,6 +21,10 @@
 
 def round_up(value, unit):
     return (value + unit - 1) // unit * unit
+
+
+def rows_from(row):
+    return slice(row, row + 8)
 
 
 def split_two(value):
@@ -137,43 +141,44 @@
     box_y = box_ref[1]
     box_z = box_ref[2]
 
-    def tile_rows(at, height, row):
-        return pl.ds(pl.multiple_of(at // LANES * height + row, 8), 8)
 
     ramps = [
         (lax.broadcasted_iota(jnp.int32, (16, LANES), 0) + group).astype(jnp.float32).astype(jnp.bfloat16)
         for group in range(0, LANES, 16)
     ]
 
-    def hot(index, hots, at):
+    def hot(index, hots, tile):
         low = jnp.broadcast_to((index & (LANES - 1)).astype(jnp.float32), (16, LANES)).astype(jnp.bfloat16)
         for group in range(LANES // 16):
-            hots[pl.ds(pl.multiple_of(at + group * 16, 16), 16), :] = jnp.where(
+            hots[tile, group * 16 : group * 16 + 16, :] = jnp.where(
                 low == ramps[group], jnp.bfloat16(1), jnp.bfloat16(0)
             )
 
+    group_parts = next(n for n in (12, 6, 4, 3, 2, 1) if pairs // LANES % n == 0)
+
     def prepare(number, carry):
-        for part in range(parts):
-            at = pl.multiple_of(number * block + part * LANES, LANES)
+        for part in range(group_parts):
+            tile = number * group_parts + part
+            at = pl.multiple_of(tile * LANES, LANES)
             here = pl.ds(at, LANES)
-            hot(pair_ref[0:1, here], first_hot, at)
-            hot(pair_ref[1:2, here], second_hot, at)
+            hot(pair_ref[0:1, here], first_hot, tile)
+            hot(pair_ref[1:2, here], second_hot, tile)
             first = picked_rows(
                 packed_ref, jnp.broadcast_to(pair_ref[0:1, here], (8, LANES)), 0, first_tiles
             )
             for c in range(3):
                 origin = first[c][0:1]
-                first_kept[tile_rows(at, 88, 48 + c * 8), :] = jnp.broadcast_to(origin, (8, LANES))
+                first_kept[tile, rows_from(48 + c * 8), :] = jnp.broadcast_to(origin, (8, LANES))
                 first[c] = first[c] - jnp.broadcast_to(origin, (8, LANES))
             first[4] = 6.0 * first[4]
             first[5] = 12.0 * first[5]
             for c in range(6):
-                first_kept[tile_rows(at, 88, c * 8), :] = first[c]
+                first_kept[tile, rows_from(c * 8), :] = first[c]
             image = jnp.broadcast_to(pair_ref[2:3, here], (8, LANES))
             step_y = jnp.where(image >= 6, 1.0, jnp.where(image >= 3, 0.0, -1.0))
             step_z = image.astype(jnp.float32) - 3.0 * step_y - 4.0
-            first_kept[tile_rows(at, 88, 72), :] = step_y * box_y
-            first_kept[tile_rows(at, 88, 80), :] = step_z * box_z
+            first_kept[tile, rows_from(72), :] = step_y * box_y
+            first_kept[tile, rows_from(80), :] = step_z * box_z
             words = [jnp.broadcast_to(word_ref[w : w + 1, here], (8, LANES)) for w in range(4)]
             low = jnp.where(sublane < 2, words[0], words[1])
             high = jnp.where(sublane < 6, words[2], words[3])
@@ -181,11 +186,11 @@
             bits = jnp.where(at + lane < total, bits, 0)
             for turn in range(8):
                 wanted = (bits & (1 << ((sublane + turn) & 7))) != 0
-                far_kept[tile_rows(at, 64, turn * 8), :] = jnp.where(wanted, 0.0, FAR_AWAY)
-                term_kept[tile_rows(at, 64, turn * 8), :] = jnp.where(wanted, reaction_term, 0.0)
+                far_kept[tile, rows_from(turn * 8), :] = jnp.where(wanted, 0.0, FAR_AWAY)
+                term_kept[tile, rows_from(turn * 8), :] = jnp.where(wanted, reaction_term, 0.0)
         return carry
 
-    lax.fori_loop(0, blocks, prepare, 0)
+    lax.fori_loop(0, pairs // LANES // group_parts, prepare, 0)
     for copy in inward[7:]:
         copy.wait()
     energy = velocity_ref[...] * velocity_ref[...] / param_ref[3:4, :]
@@ -218,19 +223,20 @@
     def fetch(number, part, slot):
         at = pl.multiple_of(number * block + part * LANES, LANES)
         here = pl.ds(at, LANES)
+        tile = number * parts + part
         second = picked_rows(
             table_ref, jnp.broadcast_to(pair_ref[1:2, here], (8, LANES)), 0, second_tiles
         )
         for c in range(3):
-            second[c] = second[c] - first_kept[tile_rows(at, 88, 48 + c * 8), :]
+            second[c] = second[c] - first_kept[tile, rows_from(48 + c * 8), :]
             if c:
-                second[c] = second[c] + first_kept[tile_rows(at, 88, 64 + c * 8), :]
+                second[c] = second[c] + first_kept[tile, rows_from(64 + c * 8), :]
         for c in range(6):
             second_got[slot * 48 + c * 8 : slot * 48 + c * 8 + 8, :] = second[c]
 
     def interact(number, part):
-        at = pl.multiple_of(number * block + part * LANES, LANES)
-        first = [first_kept[tile_rows(at, 88, c * 8), :] for c in range(6)]
+        tile = number * parts + part
+        first = [first_kept[tile, rows_from(c * 8), :] for c in range(6)]
         low = (part % 2) * 48
         charge, dispersion, repulsion = first[3], first[4], first[5]
         from_first = [None] * 3
@@ -241,11 +247,11 @@
                 moving = [pltpu.roll(m, 8 - turn, 0) for m in moving]
             delta = [moving[c] - first[c] for c in range(3)]
             radius_sq = delta[0] * delta[0] + delta[1] * delta[1] + delta[2] * delta[2]
-            inverse = lax.rsqrt(radius_sq + far_kept[tile_rows(at, 64, turn * 8), :])
+            inverse = lax.rsqrt(radius_sq + far_kept[tile, rows_from(turn * 8), :])
             inverse_sq = inverse * inverse
             cube = inverse * inverse_sq
             six = cube * cube
-            scalar = charge * moving[3] * (cube - term_kept[tile_rows(at, 64, turn * 8), :]) + (
+            scalar = charge * moving[3] * (cube - term_kept[tile, rows_from(turn * 8), :]) + (
                 repulsion * moving[5] * six - dispersion * moving[4]
             ) * (six * inverse_sq)
             for c in range(3):
@@ -277,7 +283,7 @@
                 rows.append(jnp.concatenate([
                     jnp.where(home == jnp.bfloat16(tile), pieces, jnp.bfloat16(0)) for tile in range(tiles)
                 ], axis=0))
-                columns.append(hots[pl.ds(at, LANES), :])
+                columns.append(hots[number * parts + part, :, :])
             target[...] += lax.dot_general(
                 jnp.concatenate(rows, axis=1), jnp.concatenate(columns, axis=1),
                 (((1,), (1,)), ((), ())), preferred_element_type=jnp.float32,
@@ -444,8 +450,9 @@
             f32(24, wide), f32(24, wide_far), f32(24, wide), f32(24, wide_far),
             f32(1, LANES), f32(count, 1, LANES),
             pltpu.VMEM((8, wide), jnp.int32), f32(24, wide),
-            f32(pairs // LANES * 88, LANES), f32(pairs // LANES * 64, LANES), f32(pairs // LANES * 64, LANES),
-pltpu.VMEM((pairs, LANES), jnp.bfloat16), pltpu.VMEM((pairs, LANES), jnp.bfloat16),
+            f32(pairs // LANES, 88, LANES), f32(pairs // LANES, 64, LANES), f32(pairs // LANES, 64, LANES),
+pltpu.VMEM((pairs // LANES, LANES, LANES), jnp.bfloat16),
+            pltpu.VMEM((pairs // LANES, LANES, LANES), jnp.bfloat16),
             f32(96, LANES), f32(block // LANES * 24, LANES), f32(block // LANES * 24, LANES),
             f32(wide // LANES * 48, LANES), f32(wide_slots // LANES * 48, LANES), f32(24, LANES),
             pltpu.SemaphoreType.DMA((9,)), pltpu.SemaphoreType.DMA((4,)), pltpu.SemaphoreType.DMA((4,)),

time: 27.2 us -> 26.9 us (0.989)
  no operation moved by 1% of the time
where the time goes in v5:
time: 26.9 us; the launch traced here: 26.8 us
  Pallas kernels  25.4 us (94%)
  between operations  1.33 us (5%)
    pallas_call x1, Pallas kernels, on_device(): pl.pallas_call(functools.partial(step_kernel, count=count, clusters=clust...  24.6 us
    pallas_call x1, Pallas kernels, on_device(): pl.pallas_call(functools.partial(final_kernel, clusters=clusters), name='...  0.81 us

profile of v5, /device:TPU:0, one launch (start us, length us, event | category | flops | bytes accessed | tf_op | source)
XLA Modules:
  0.0 26.8 jit_solution(15921791118509763329)
XLA Ops:
  1.3 0.0 copy-start
  1.3 0.0 copy-start.1
  1.3 0.0 copy-start.2
  1.3 24.6 %step_kernel.1 = (f32[24,256]{1,0:T(8,128)S(1)}, f32[4,128]{1,0:T(4,128)S(1)}) custom-call(f32[3]{0:T(128)} %box_in.1, f32[4]{0:T(128)} %extended_in.1, s32[1]{0:T(128)S(6)} %copy.13.count_in, f32[3,1536]{1,0:T(4,128)} %position_ref.1, f32[3,1536]{1,0:T(4,128)} %velocity_ref.1, f32[4,1536]{1,0:T(4,128)} %param_ref.1, s32[3,16896]{1,0:T(4,128)} %pair_in.1, ...), custom_call_target="tpu_custom_call" | custom-call | tf_op jit(solution)/shard_map/step_kernel/pallas_call | solution.py:435
  25.9 0.0 copy-done
  25.9 0.0 copy-done.1
  25.9 0.0 copy-done.2
  26.0 0.8 %final_kernel.1 = (f32[3,1536]{1,0:T(4,128)}, f32[3,1536]{1,0:T(4,128)}, f32[3,1536]{1,0:T(4,128)}, f32[1,4]{1,0:T(1,128)}) custom-call(f32[24,256]{1,0:T(8,128)S(1)} %get-tuple-element.10.folded_ref, f32[4,128]{1,0:T(4,128)S(1)} %get-tuple-element.11.rate_ref, f32[3,1536]{1,0:T(4,128)S(1)} %copy-done, f32[3,1536]{1,0:T(4,128)S(1)} %copy-done.1, ...), custom_call_target="tpu_custom_call" | custom-call | tf_op jit(solution)/shard_map/final_kernel/pallas_call | solution.py:468
Async XLA Ops:
  1.3 24.7 %copy-start = (f32[3,1536]{1,0:T(4,128)S(1)}, f32[3,1536]{1,0:T(4,128)}, u32[]{:S(2)}) copy-start(f32[3,1536]{1,0:T(4,128)} %position_ref.1) | copy-start | bytes 55300
  1.3 24.7 %copy-start.1 = (f32[3,1536]{1,0:T(4,128)S(1)}, f32[3,1536]{1,0:T(4,128)}, u32[]{:S(2)}) copy-start(f32[3,1536]{1,0:T(4,128)} %velocity_ref.1) | copy-start | bytes 55300
  1.3 24.7 %copy-start.2 = (f32[4,1536]{1,0:T(4,128)S(1)}, f32[4,1536]{1,0:T(4,128)}, u32[]{:S(2)}) copy-start(f32[4,1536]{1,0:T(4,128)} %param_ref.1) | copy-start | bytes 73732

commit v6 on v5

--- a/solution.py
+++ b/solution.py
@@ -167,25 +167,28 @@
                 packed_ref, jnp.broadcast_to(pair_ref[0:1, here], (8, LANES)), 0, first_tiles
             )
             for c in range(3):
-                origin = first[c][0:1]
-                first_kept[tile, rows_from(48 + c * 8), :] = jnp.broadcast_to(origin, (8, LANES))
-                first[c] = first[c] - jnp.broadcast_to(origin, (8, LANES))
+                origin = jnp.broadcast_to(first[c][0:1], (8, LANES))
+                first_kept[tile, rows_from(384 + c * 8), :] = origin
+                first[c] = first[c] - origin
             first[4] = 6.0 * first[4]
             first[5] = 12.0 * first[5]
-            for c in range(6):
-                first_kept[tile, rows_from(c * 8), :] = first[c]
+            for turn in range(8):
+                for c in range(6):
+                    turned = pltpu.roll(first[c], 8 - turn, 0) if turn else first[c]
+                    first_kept[tile, rows_from(turn * 48 + c * 8), :] = turned
             image = jnp.broadcast_to(pair_ref[2:3, here], (8, LANES))
             step_y = jnp.where(image >= 6, 1.0, jnp.where(image >= 3, 0.0, -1.0))
             step_z = image.astype(jnp.float32) - 3.0 * step_y - 4.0
-            first_kept[tile, rows_from(72), :] = step_y * box_y
-            first_kept[tile, rows_from(80), :] = step_z * box_z
+            first_kept[tile, rows_from(408), :] = step_y * box_y
+            first_kept[tile, rows_from(416), :] = step_z * box_z
             words = [jnp.broadcast_to(word_ref[w : w + 1, here], (8, LANES)) for w in range(4)]
             low = jnp.where(sublane < 2, words[0], words[1])
             high = jnp.where(sublane < 6, words[2], words[3])
             bits = jnp.where(sublane < 4, low, high) >> (8 * (sublane & 1))
             bits = jnp.where(at + lane < total, bits, 0)
             for turn in range(8):
-                wanted = (bits & (1 << ((sublane + turn) & 7))) != 0
+                turned = pltpu.roll(bits, 8 - turn, 0) if turn else bits
+                wanted = (turned & (1 << sublane)) != 0
                 far_kept[tile, rows_from(turn * 8), :] = jnp.where(wanted, 0.0, FAR_AWAY)
                 term_kept[tile, rows_from(turn * 8), :] = jnp.where(wanted, reaction_term, 0.0)
         return carry
@@ -228,44 +231,41 @@
             table_ref, jnp.broadcast_to(pair_ref[1:2, here], (8, LANES)), 0, second_tiles
         )
         for c in range(3):
-            second[c] = second[c] - first_kept[tile, rows_from(48 + c * 8), :]
+            second[c] = second[c] - first_kept[tile, rows_from(384 + c * 8), :]
             if c:
-                second[c] = second[c] + first_kept[tile, rows_from(64 + c * 8), :]
+                second[c] = second[c] + first_kept[tile, rows_from(400 + c * 8), :]
         for c in range(6):
             second_got[slot * 48 + c * 8 : slot * 48 + c * 8 + 8, :] = second[c]
 
     def interact(number, part):
         tile = number * parts + part
-        first = [first_kept[tile, rows_from(c * 8), :] for c in range(6)]
         low = (part % 2) * 48
-        charge, dispersion, repulsion = first[3], first[4], first[5]
+        second = [second_got[low + c * 8 : low + c * 8 + 8, :] for c in range(6)]
         from_first = [None] * 3
         onto_second = [None] * 3
         for turn in range(7, -1, -1):
-            moving = [second_got[low + c * 8 : low + c * 8 + 8, :] for c in range(6)]
-            if turn:
-                moving = [pltpu.roll(m, 8 - turn, 0) for m in moving]
-            delta = [moving[c] - first[c] for c in range(3)]
+            first = [first_kept[tile, rows_from(turn * 48 + c * 8), :] for c in range(6)]
+            delta = [second[c] - first[c] for c in range(3)]
             radius_sq = delta[0] * delta[0] + delta[1] * delta[1] + delta[2] * delta[2]
             inverse = lax.rsqrt(radius_sq + far_kept[tile, rows_from(turn * 8), :])
             inverse_sq = inverse * inverse
             cube = inverse * inverse_sq
             six = cube * cube
-            scalar = charge * moving[3] * (cube - term_kept[tile, rows_from(turn * 8), :]) + (
-                repulsion * moving[5] * six - dispersion * moving[4]
+            scalar = first[3] * second[3] * (cube - term_kept[tile, rows_from(turn * 8), :]) + (
+                first[5] * second[5] * six - first[4] * second[4]
             ) * (six * inverse_sq)
             for c in range(3):
                 force = scalar * delta[c]
-                if from_first[c] is None:
+                if onto_second[c] is None:
                     from_first[c] = force
                     onto_second[c] = force
                 else:
-                    from_first[c] = from_first[c] + force
-                    onto_second[c] = pltpu.roll(onto_second[c], 1, 0) + force
+                    from_first[c] = pltpu.roll(from_first[c], 1, 0) + force
+                    onto_second[c] = onto_second[c] + force
         for c in range(3):
             first_terms[part * 24 + c * 8 : part * 24 + c * 8 + 8, :] = from_first[c]
             second_terms[part * 24 + c * 8 : part * 24 + c * 8 + 8, :] = onto_second[c]
-        return [onto_second[c] * moving[c] - from_first[c] * first[c] for c in range(3)]
+        return [onto_second[c] * second[c] - from_first[c] * first[c] for c in range(3)]
 
     def spread(number):
         for target, terms, row, hots, tiles in (
@@ -423,7 +423,7 @@
     slots = 2 * clusters + far_clusters
     pairs = pair_list.shape[1]
     count = lax.axis_size("gx")
-    block = next(b for b in (768, 512, 384, 256, 128) if pairs % b == 0)
+    block = next(b for b in (768, 512, 256) if pairs % b == 0)
     wide = round_up(clusters, LANES)
     wide_far = round_up(far_clusters, LANES)
     wide_slots = round_up(slots, LANES)
@@ -450,7 +450,7 @@
             f32(24, wide), f32(24, wide_far), f32(24, wide), f32(24, wide_far),
             f32(1, LANES), f32(count, 1, LANES),
             pltpu.VMEM((8, wide), jnp.int32), f32(24, wide),
-            f32(pairs // LANES, 88, LANES), f32(pairs // LANES, 64, LANES), f32(pairs // LANES, 64, LANES),
+            f32(pairs // LANES, 424, LANES), f32(pairs // LANES, 64, LANES), f32(pairs // LANES, 64, LANES),
 pltpu.VMEM((pairs // LANES, LANES, LANES), jnp.bfloat16),
             pltpu.VMEM((pairs // LANES, LANES, LANES), jnp.bfloat16),
             f32(96, LANES), f32(block // LANES * 24, LANES), f32(block // LANES * 24, LANES),
@@ -459,7 +459,7 @@
             pltpu.SemaphoreType.DMA((count,)), pltpu.SemaphoreType.DMA((count,)),
         ],
         compiler_params=pltpu.CompilerParams(
-            collective_id=0, has_side_effects=True, vmem_limit_bytes=32 * 1024 * 1024
+            collective_id=0, has_side_effects=True, vmem_limit_bytes=48 * 1024 * 1024
         ),
     )(
         pinned(box_lengths), pinned(extended_variables), pair_count, pinned(positions), pinned(velocities),

time: 26.9 us -> 26.8 us (level)
  no operation moved by 1% of the time
where the time goes in v6:
time: 26.8 us; the launch traced here: 26.7 us
  Pallas kernels  25.3 us (94%)
  between operations  1.33 us (5%)
    pallas_call x1, Pallas kernels, on_device(): pl.pallas_call(functools.partial(step_kernel, count=count, clusters=clust...  24.5 us
    pallas_call x1, Pallas kernels, on_device(): pl.pallas_call(functools.partial(final_kernel, clusters=clusters), name='...  0.81 us

profile of v6, /device:TPU:0, one launch (start us, length us, event | category | flops | bytes accessed | tf_op | source)
XLA Modules:
  0.0 26.7 jit_solution(1919239250913069236)
XLA Ops:
  1.3 0.0 copy-start
  1.3 0.0 copy-start.1
  1.3 0.0 copy-start.2
  1.3 24.5 %step_kernel.1 = (f32[24,256]{1,0:T(8,128)S(1)}, f32[4,128]{1,0:T(4,128)S(1)}) custom-call(f32[3]{0:T(128)} %box_in.1, f32[4]{0:T(128)} %extended_in.1, s32[1]{0:T(128)S(6)} %copy.13.count_in, f32[3,1536]{1,0:T(4,128)} %position_ref.1, f32[3,1536]{1,0:T(4,128)} %velocity_ref.1, f32[4,1536]{1,0:T(4,128)} %param_ref.1, s32[3,16896]{1,0:T(4,128)} %pair_in.1, ...), custom_call_target="tpu_custom_call" | custom-call | tf_op jit(solution)/shard_map/step_kernel/pallas_call | solution.py:435
  25.8 0.0 copy-done
  25.9 0.0 copy-done.1
  25.9 0.0 copy-done.2
  25.9 0.8 %final_kernel.1 = (f32[3,1536]{1,0:T(4,128)}, f32[3,1536]{1,0:T(4,128)}, f32[3,1536]{1,0:T(4,128)}, f32[1,4]{1,0:T(1,128)}) custom-call(f32[24,256]{1,0:T(8,128)S(1)} %get-tuple-element.10.folded_ref, f32[4,128]{1,0:T(4,128)S(1)} %get-tuple-element.11.rate_ref, f32[3,1536]{1,0:T(4,128)S(1)} %copy-done, f32[3,1536]{1,0:T(4,128)S(1)} %copy-done.1, ...), custom_call_target="tpu_custom_call" | custom-call | tf_op jit(solution)/shard_map/final_kernel/pallas_call | solution.py:468
Async XLA Ops:
  1.3 24.6 %copy-start = (f32[3,1536]{1,0:T(4,128)S(1)}, f32[3,1536]{1,0:T(4,128)}, u32[]{:S(2)}) copy-start(f32[3,1536]{1,0:T(4,128)} %position_ref.1) | copy-start | bytes 55300
  1.3 24.6 %copy-start.1 = (f32[3,1536]{1,0:T(4,128)S(1)}, f32[3,1536]{1,0:T(4,128)}, u32[]{:S(2)}) copy-start(f32[3,1536]{1,0:T(4,128)} %velocity_ref.1) | copy-start | bytes 55300
  1.3 24.6 %copy-start.2 = (f32[4,1536]{1,0:T(4,128)S(1)}, f32[4,1536]{1,0:T(4,128)}, u32[]{:S(2)}) copy-start(f32[4,1536]{1,0:T(4,128)} %param_ref.1) | copy-start | bytes 73732

commit v7 on v6

--- a/solution.py
+++ b/solution.py
@@ -285,7 +285,7 @@
                 ], axis=0))
                 columns.append(hots[number * parts + part, :, :])
             target[...] += lax.dot_general(
-                jnp.concatenate(rows, axis=1), jnp.concatenate(columns, axis=1),
+                jnp.concatenate(columns, axis=1), jnp.concatenate(rows, axis=1),
                 (((1,), (1,)), ((), ())), preferred_element_type=jnp.float32,
             )
 
@@ -331,8 +331,13 @@
         return carry
 
     def joined(ref, tiles):
+        value = ref[...]
+        wide = round_up(value.shape[1], LANES)
+        if wide > value.shape[1]:
+            value = jnp.concatenate([value, jnp.zeros((LANES, wide - value.shape[1]), jnp.float32)], axis=1)
+        value = value.T
         return jnp.concatenate([
-            ref[tile * 48 : tile * 48 + 24, :] + ref[tile * 48 + 24 : tile * 48 + 48, :]
+            value[tile * 48 : tile * 48 + 24, :] + value[tile * 48 + 24 : tile * 48 + 48, :]
             for tile in range(tiles)
         ], axis=1)
 
@@ -454,7 +459,7 @@
 pltpu.VMEM((pairs // LANES, LANES, LANES), jnp.bfloat16),
             pltpu.VMEM((pairs // LANES, LANES, LANES), jnp.bfloat16),
             f32(96, LANES), f32(block // LANES * 24, LANES), f32(block // LANES * 24, LANES),
-            f32(wide // LANES * 48, LANES), f32(wide_slots // LANES * 48, LANES), f32(24, LANES),
+            f32(LANES, wide // LANES * 48), f32(LANES, wide_slots // LANES * 48), f32(24, LANES),
             pltpu.SemaphoreType.DMA((9,)), pltpu.SemaphoreType.DMA((4,)), pltpu.SemaphoreType.DMA((4,)),
             pltpu.SemaphoreType.DMA((count,)), pltpu.SemaphoreType.DMA((count,)),
         ],

time: 26.8 us -> 27 us (level)
  no operation moved by 1% of the time
where the time goes in v7:
time: 27 us; the launch traced here: 26.8 us
  Pallas kernels  25.5 us (94%)
  between operations  1.33 us (5%)
    pallas_call x1, Pallas kernels, on_device(): pl.pallas_call(functools.partial(step_kernel, count=count, clusters=clust...  24.7 us
    pallas_call x1, Pallas kernels, on_device(): pl.pallas_call(functools.partial(final_kernel, clusters=clusters), name='...  0.81 us

profile of v7, /device:TPU:0, one launch (start us, length us, event | category | flops | bytes accessed | tf_op | source)
XLA Modules:
  0.0 26.8 jit_solution(10899230979791140890)
XLA Ops:
  1.3 0.0 copy-start
  1.3 0.0 copy-start.1
  1.3 0.0 copy-start.2
  1.3 24.7 %step_kernel.1 = (f32[24,256]{1,0:T(8,128)S(1)}, f32[4,128]{1,0:T(4,128)S(1)}) custom-call(f32[3]{0:T(128)} %box_in.1, f32[4]{0:T(128)} %extended_in.1, s32[1]{0:T(128)S(6)} %copy.13.count_in, f32[3,1536]{1,0:T(4,128)} %position_ref.1, f32[3,1536]{1,0:T(4,128)} %velocity_ref.1, f32[4,1536]{1,0:T(4,128)} %param_ref.1, s32[3,16896]{1,0:T(4,128)} %pair_in.1, ...), custom_call_target="tpu_custom_call" | custom-call | tf_op jit(solution)/shard_map/step_kernel/pallas_call | solution.py:440
  26.0 0.0 copy-done
  26.0 0.0 copy-done.1
  26.0 0.0 copy-done.2
  26.0 0.8 %final_kernel.1 = (f32[3,1536]{1,0:T(4,128)}, f32[3,1536]{1,0:T(4,128)}, f32[3,1536]{1,0:T(4,128)}, f32[1,4]{1,0:T(1,128)}) custom-call(f32[24,256]{1,0:T(8,128)S(1)} %get-tuple-element.10.folded_ref, f32[4,128]{1,0:T(4,128)S(1)} %get-tuple-element.11.rate_ref, f32[3,1536]{1,0:T(4,128)S(1)} %copy-done, f32[3,1536]{1,0:T(4,128)S(1)} %copy-done.1, ...), custom_call_target="tpu_custom_call" | custom-call | tf_op jit(solution)/shard_map/final_kernel/pallas_call | solution.py:473
Async XLA Ops:
  1.3 24.7 %copy-start = (f32[3,1536]{1,0:T(4,128)S(1)}, f32[3,1536]{1,0:T(4,128)}, u32[]{:S(2)}) copy-start(f32[3,1536]{1,0:T(4,128)} %position_ref.1) | copy-start | bytes 55300
  1.3 24.7 %copy-start.1 = (f32[3,1536]{1,0:T(4,128)S(1)}, f32[3,1536]{1,0:T(4,128)}, u32[]{:S(2)}) copy-start(f32[3,1536]{1,0:T(4,128)} %velocity_ref.1) | copy-start | bytes 55300
  1.3 24.7 %copy-start.2 = (f32[4,1536]{1,0:T(4,128)S(1)}, f32[4,1536]{1,0:T(4,128)}, u32[]{:S(2)}) copy-start(f32[4,1536]{1,0:T(4,128)} %param_ref.1) | copy-start | bytes 73732
